TPU v7x, 256 devices: a whole 4x4x8 slice. The times are simulated.
256 devices in a mesh: lat: 4 (over y), lon: 64 (over x, z, core).
Axes of the slice: x: 4, y: 4, z: 8, core: 2. Of those that a mesh axis runs over, the one named last changes fastest.
Arguments:
- right_side: float32 [512, 8192], P('lat', 'lon'), may hold values from -8 to 8
- surface_term: float32 [512, 8192], P('lat', 'lon'), may hold values from 0.0002 to 0.002
- east_coupling: float32 [512, 8192], P('lat', 'lon'), may hold values from 0.3 to 3
- north_coupling: float32 [512, 8192], P('lat', 'lon'), may hold values from 0.3 to 3
- neast_coupling: float32 [512, 8192], P('lat', 'lon'), may hold values from 0.1 to 0.5
- nwest_coupling: float32 [512, 8192], P('lat', 'lon'), may hold values from 0.1 to 0.5
- land_sea: int32 [512, 8192], P('lat', 'lon'), may hold values from 0 to 1, as said below
- fold_map: int32 [8192], P('lon'), may hold values from 0 to 8191, as said below
Outputs:
- solution: float32 [512, 8192], P('lat', 'lon')
- residual: float32 [512, 8192], P('lat', 'lon')
Inputs may be any that keep to these rules, and one draw needn't show every extreme that they name: fold_map[j] = (c - j) mod 8192 for one odd c: an involution of the columns with no fixed point. land_sea is 0 or 1; land lies in bands of 8 columns, each over one range of rows.
All inputs are finite; a program needn't handle non-finite values.
Results may differ from a plain program's by a relative error of at most 0.0015.
Values sent between devices are 32-bit elements.
A program may use at most 64 MiB of HBM per device.

v0:
```python
import functools

import jax
import jax.numpy as jnp
from jax import lax
from jax.sharding import Mesh
from jax.sharding import PartitionSpec as P

ITERS = 8
LAT_LON = ("lat", "lon_0", "lon_1", "lon_2")
LON = ("lon_0", "lon_1", "lon_2")


OFFSETS = ((0, 1), (0, -1), (1, 0), (-1, 0), (1, 1), (-1, -1), (1, -1), (-1, 1))
COUPLINGS = (
    (1, 0, 0),
    (1, 0, -1),
    (2, 0, 0),
    (2, -1, 0),
    (3, 0, 0),
    (3, -1, -1),
    (4, 0, 0),
    (4, -1, 1),
)


def one_axis_at_a_time(shard, axes):
    return functools.reduce(lax.psum, axes, shard)


def with_halo(shard, sides, width):
    for axis, dim in sides:
        size, length = (lax.axis_size(axis), shard.shape[dim])
        up = [(i, (i + 1) % size) for i in range(size)]
        down = [(j, i) for i, j in up]
        last = lax.slice_in_dim(shard, length - width, length, axis=dim)
        first = lax.slice_in_dim(shard, 0, width, axis=dim)
        before = lax.ppermute(last, axis, up)
        after = lax.ppermute(first, axis, down)
        shard = jnp.concatenate([before, shard, after], axis=dim)
    return shard


def joined_along(blocks, dim):
    blocks = jnp.moveaxis(blocks, 0, dim)
    shape = blocks.shape
    return blocks.reshape(*shape[:dim], shape[dim] * shape[dim + 1], *shape[dim + 2 :])


def copy_for_each(shard, axis):
    copies = jnp.broadcast_to(shard, (lax.axis_size(axis), *shard.shape))
    return lax.all_to_all(copies, axis, split_axis=0, concat_axis=0, tiled=True)


def gathered_copies(shard, axis, dim):
    return joined_along(copy_for_each(shard, axis), dim)


def interior(padded, row_step, col_step):
    row_count = padded.shape[-2] - 2
    col_count = padded.shape[-1] - 2
    return padded[
        ..., 1 + row_step : 1 + row_step + row_count, 1 + col_step : 1 + col_step + col_count
    ]


def stencil_weights(padded):
    ocean_pad = padded[0]
    centre = interior(ocean_pad, 0, 0)
    weight_list = []
    open_sum = jnp.zeros_like(centre)
    for (layer_index, row_step, col_step), (row_off, col_off) in zip(COUPLINGS, OFFSETS):
        edge_value = interior(padded[layer_index], row_step, col_step)
        weight_list.append(edge_value * centre * interior(ocean_pad, row_off, col_off))
        open_sum = open_sum + edge_value
    return (jnp.stack(weight_list), open_sum)


def neighbour_sum(weights, padded_field):
    accumulated = jnp.zeros_like(weights[0])
    for position, (row_off, col_off) in enumerate(OFFSETS):
        accumulated = accumulated + weights[position] * interior(padded_field, row_off, col_off)
    return accumulated


def shift_down(values, stride, fill):
    pad_shape = values.shape[:-2] + (stride, values.shape[-1])
    filler = jnp.full(pad_shape, fill, values.dtype)
    return jnp.concatenate([filler, values[..., :-stride, :]], axis=-2)


def shift_up(values, stride, fill):
    pad_shape = values.shape[:-2] + (stride, values.shape[-1])
    filler = jnp.full(pad_shape, fill, values.dtype)
    return jnp.concatenate([values[..., stride:, :], filler], axis=-2)


def reduction_plan(lower_band, middle_band, upper_band):
    factors = []
    stride = 1
    while stride < middle_band.shape[-2]:
        left_factor = lower_band / shift_down(middle_band, stride, 1.0)
        right_factor = upper_band / shift_up(middle_band, stride, 1.0)
        new_middle = (
            middle_band
            - shift_down(upper_band, stride, 0.0) * left_factor
            - shift_up(lower_band, stride, 0.0) * right_factor
        )
        lower_band = -shift_down(lower_band, stride, 0.0) * left_factor
        upper_band = -shift_up(upper_band, stride, 0.0) * right_factor
        middle_band = new_middle
        factors.append((left_factor, right_factor))
        stride = stride * 2
    return (factors, middle_band)


def reduce_apply(factors, pivots, values):
    stride = 1
    for left_factor, right_factor in factors:
        values = (
            values
            - left_factor * shift_down(values, stride, 0.0)
            - right_factor * shift_up(values, stride, 0.0)
        )
        stride = stride * 2
    return values / pivots


def reduced_inverse(all_responses, lat_count):
    order_count = 2 * lat_count
    col_count = all_responses.shape[-1]
    identity = jnp.broadcast_to(
        jnp.eye(order_count, dtype=jnp.float32)[:, :, None], (order_count, order_count, col_count)
    )
    matrix = identity
    for block_index in range(lat_count):
        if block_index > 0:
            matrix = matrix.at[2 * block_index, 2 * block_index - 1].set(
                -all_responses[4 * block_index]
            )
            matrix = matrix.at[2 * block_index + 1, 2 * block_index - 1].set(
                -all_responses[4 * block_index + 1]
            )
        if block_index < lat_count - 1:
            matrix = matrix.at[2 * block_index, 2 * block_index + 2].set(
                -all_responses[4 * block_index + 2]
            )
            matrix = matrix.at[2 * block_index + 1, 2 * block_index + 2].set(
                -all_responses[4 * block_index + 3]
            )
    inverse = identity
    for pivot_row in range(order_count):
        pivot_value = matrix[pivot_row, pivot_row]
        scaled_matrix = matrix[pivot_row] / pivot_value
        scaled_inverse = inverse[pivot_row] / pivot_value
        pivot_column = matrix[:, pivot_row]
        matrix = matrix - pivot_column[:, None] * scaled_matrix[None]
        inverse = inverse - pivot_column[:, None] * scaled_inverse[None]
        matrix = matrix.at[pivot_row].set(scaled_matrix)
        inverse = inverse.at[pivot_row].set(scaled_inverse)
    return inverse


def both_products(residual, precond, image_field):
    return (
        one_axis_at_a_time(jnp.sum(residual * precond), LAT_LON),
        one_axis_at_a_time(jnp.sum(image_field * precond), LAT_LON),
    )


def shards(
    right_side,
    surface_term,
    east_coupling,
    north_coupling,
    neast_coupling,
    nwest_coupling,
    land_sea,
    fold_map,
):
    row_count, col_count = right_side.shape
    lat_count = lax.axis_size("lat")
    lat_place = lax.axis_index("lat")
    is_top = (lat_place == lat_count - 1).astype(jnp.float32)
    is_bottom = (lat_place == 0).astype(jnp.float32)
    ocean = land_sea.astype(jnp.float32)
    row_ids = lax.broadcasted_iota(jnp.int32, (row_count, col_count), 0)
    top_row = jnp.where(row_ids == row_count - 1, is_top, 0.0)
    open_rows = 1.0 - top_row
    stacked = jnp.stack(
        [
            ocean,
            east_coupling,
            north_coupling * open_rows,
            neast_coupling * open_rows,
            nwest_coupling * open_rows,
        ]
    )
    padded = with_halo(stacked, (("lat", 1), (LON, 2)), 1)
    pad_rows = lax.broadcasted_iota(jnp.int32, (row_count + 2, 1), 0)
    closed = (pad_rows == 0) & (lat_place == 0) | (pad_rows == row_count + 1) & (
        lat_place == lat_count - 1
    )
    padded = jnp.where(closed[None], 0.0, padded)
    weights, open_sum = stencil_weights(padded)
    top_pair = jnp.stack([north_coupling[-1], ocean[-1]])
    whole_top = gathered_copies(top_pair, LON, 1)
    partner = jnp.take(whole_top, fold_map, axis=1)
    fold_open = 0.5 * (north_coupling[-1] + partner[0]) * is_top
    fold_weight = fold_open * ocean[-1] * partner[1]
    diagonal = ocean * (surface_term + open_sum + top_row * fold_open[None]) + (1.0 - ocean)
    line_diagonal = ocean * (surface_term + weights[2] + weights[3]) + (1.0 - ocean)

    def operate(field, south_row, north_row):
        extended = jnp.concatenate([south_row[None], field, north_row[None]], axis=0)
        padded_field = with_halo(extended, ((LON, 1),), 1)
        whole_row = gathered_copies(field[-1], LON, 0)
        fold_term = fold_weight * jnp.take(whole_row, fold_map)
        return diagonal * field - neighbour_sum(weights, padded_field) - top_row * fold_term[None]

    local_lower = jnp.where(row_ids > 0, -weights[3], 0.0)
    local_upper = jnp.where(row_ids < row_count - 1, -weights[2], 0.0)
    factors, pivots = reduction_plan(local_lower, line_diagonal, local_upper)
    boundary = jnp.stack(
        [
            jnp.where(row_ids == 0, weights[3], 0.0),
            jnp.where(row_ids == row_count - 1, weights[2], 0.0),
        ]
    )
    responses = reduce_apply(factors, pivots, boundary)
    response_ends = jnp.stack(
        [responses[0, 0], responses[0, -1], responses[1, 0], responses[1, -1]]
    )
    all_responses = gathered_copies(response_ends, "lat", 0)
    coupling_inverse = reduced_inverse(all_responses, lat_count)
    below_index = jnp.maximum(2 * lat_place - 1, 0)
    above_index = jnp.minimum(2 * lat_place + 2, 2 * lat_count - 1)

    def precondition(residual_now):
        local_part = reduce_apply(factors, pivots, residual_now)
        end_values = jnp.stack([local_part[0], local_part[-1]])
        gathered_ends = lax.all_gather(end_values, "lat", axis=0, tiled=True)
        boundary_values = jnp.sum(coupling_inverse * gathered_ends[None], axis=1)
        below_value = lax.dynamic_index_in_dim(boundary_values, below_index, 0, keepdims=False)
        above_value = lax.dynamic_index_in_dim(boundary_values, above_index, 0, keepdims=False)
        result = local_part + below_value[None] * responses[0] + above_value[None] * responses[1]
        return (result, below_value * (1.0 - is_bottom), above_value * (1.0 - is_top))

    residual = ocean * right_side
    precond, south_now, north_now = precondition(residual)
    image_field = operate(precond, south_now, north_now)
    product_now, curvature = both_products(residual, precond, image_field)
    step_length = product_now / curvature
    direction = precond
    along_field = image_field
    solution = step_length * direction
    residual = residual - step_length * along_field
    for iteration in range(1, ITERS):
        precond, south_now, north_now = precondition(residual)
        image_field = operate(precond, south_now, north_now)
        product_next, curvature = both_products(residual, precond, image_field)
        ratio_next = product_next / product_now
        step_length = product_next / (curvature - ratio_next * product_next / step_length)
        direction = precond + ratio_next * direction
        along_field = image_field + ratio_next * along_field
        solution = solution + step_length * direction
        residual = residual - step_length * along_field
        product_now = product_next
    return (solution, residual)


def solution(mesh):
    finer = Mesh(
        mesh.devices.reshape(mesh.shape["lat"], 4, 8, 2), ("lat", "lon_0", "lon_1", "lon_2")
    )
    placed = (
        P("lat", LON),
        P("lat", LON),
        P("lat", LON),
        P("lat", LON),
        P("lat", LON),
        P("lat", LON),
        P("lat", LON),
        P(LON),
    )
    return jax.shard_map(
        shards,
        mesh=finer,
        in_specs=placed,
        out_specs=(P("lat", LON), P("lat", LON)),
        check_vma=False,
    )
```

profile of v0, /device:TPU:1, one launch (start us, length us, event | category | flops | bytes accessed | tf_op | source)
XLA Modules:
  0.0 649.1 jit_solution(12013515594875392302)
XLA Ops:
  50.9 12.0 %all-to-all-start.2 = ((f32[64,1,128]{2,1,0:T(1,128)}), f32[64,1,128]{2,1,0:T(1,128)S(1)}, u32[]{:S(2)}, u32[]{:S(2)}) async-start(f32[64,1,128]{2,1,0:T(1,128)} %broadcast_in_dim.94), calls=%async_computation.2 | async-start | bytes 65536 | tf_op jit(solution)/shard_map/all_to_all | solution.py:52
  109.5 11.9 %all-reduce.173 = (f32[]{:T(128)}, f32[]{:T(128)}) all-reduce(f32[]{:T(128)} %get-tuple-element.385, f32[]{:T(128)} %get-tuple-element.386), channel_id=1, replica_groups=mesh['lat'=4,'lon_0'=4,'lon_1'=8,'lon_2'=2] {'lon_1'}, use_global_device_ids=true, to_apply=%region_5.6 | all-reduce | flops 2 | bytes 16 | tf_op jit(solution)/shard_map/psum | solution.py:28
  121.3 10.5 %all-reduce.197 = (f32[]{:T(128)}, f32[]{:T(128)}) all-reduce(f32[]{:T(128)} %get-tuple-element.369, f32[]{:T(128)} %get-tuple-element.370), channel_id=1, replica_groups=mesh['lat'=4,'lon_0'=4,'lon_1'=8,'lon_2'=2] {'lon_2'}, use_global_device_ids=true, to_apply=%region_6.7 | all-reduce | flops 2 | bytes 16 | tf_op jit(solution)/shard_map/psum | solution.py:28
  154.6 9.2 %all-to-all-done.3 = f32[64,1,128]{2,1,0:T(1,128)S(1)} async-done(((f32[64,1,128]{2,1,0:T(1,128)}), f32[64,1,128]{2,1,0:T(1,128)S(1)}, u32[]{:S(2)}, u32[]{:S(2)}) %all-to-all-start.3) | async-done | bytes 32800 | tf_op jit(solution)/shard_map/all_to_all | solution.py:52
  179.9 11.7 %all-reduce.172 = (f32[]{:T(128)}, f32[]{:T(128)}) all-reduce(f32[]{:T(128)} %get-tuple-element.383, f32[]{:T(128)} %get-tuple-element.384), channel_id=1, replica_groups=mesh['lat'=4,'lon_0'=4,'lon_1'=8,'lon_2'=2] {'lon_1'}, use_global_device_ids=true, to_apply=%region_16.18 | all-reduce | flops 2 | bytes 16 | tf_op jit(solution)/shard_map/psum | solution.py:28
  191.6 11.0 %all-reduce.196 = (f32[]{:T(128)}, f32[]{:T(128)}) all-reduce(f32[]{:T(128)} %get-tuple-element.367, f32[]{:T(128)} %get-tuple-element.368), channel_id=1, replica_groups=mesh['lat'=4,'lon_0'=4,'lon_1'=8,'lon_2'=2] {'lon_2'}, use_global_device_ids=true, to_apply=%region_17.19 | all-reduce | flops 2 | bytes 16 | tf_op jit(solution)/shard_map/psum | solution.py:28
  228.8 9.2 %all-to-all-done.4 = f32[64,1,128]{2,1,0:T(1,128)S(1)} async-done(((f32[64,1,128]{2,1,0:T(1,128)}), f32[64,1,128]{2,1,0:T(1,128)S(1)}, u32[]{:S(2)}, u32[]{:S(2)}) %all-to-all-start.4) | async-done | bytes 32800 | tf_op jit(solution)/shard_map/all_to_all | solution.py:52
  253.9 11.6 %all-reduce.171 = (f32[]{:T(128)}, f32[]{:T(128)}) all-reduce(f32[]{:T(128)} %get-tuple-element.381, f32[]{:T(128)} %get-tuple-element.382), channel_id=1, replica_groups=mesh['lat'=4,'lon_0'=4,'lon_1'=8,'lon_2'=2] {'lon_1'}, use_global_device_ids=true, to_apply=%region_27.29 | all-reduce | flops 2 | bytes 16 | tf_op jit(solution)/shard_map/psum | solution.py:28
  265.6 10.9 %all-reduce.195 = (f32[]{:T(128)}, f32[]{:T(128)}) all-reduce(f32[]{:T(128)} %get-tuple-element.365, f32[]{:T(128)} %get-tuple-element.366), channel_id=1, replica_groups=mesh['lat'=4,'lon_0'=4,'lon_1'=8,'lon_2'=2] {'lon_2'}, use_global_device_ids=true, to_apply=%region_28.30 | all-reduce | flops 2 | bytes 16 | tf_op jit(solution)/shard_map/psum | solution.py:28
  302.3 9.2 %all-to-all-done.5 = f32[64,1,128]{2,1,0:T(1,128)S(1)} async-done(((f32[64,1,128]{2,1,0:T(1,128)}), f32[64,1,128]{2,1,0:T(1,128)S(1)}, u32[]{:S(2)}, u32[]{:S(2)}) %all-to-all-start.5) | async-done | bytes 32800 | tf_op jit(solution)/shard_map/all_to_all | solution.py:52
  327.5 11.7 %all-reduce.170 = (f32[]{:T(128)}, f32[]{:T(128)}) all-reduce(f32[]{:T(128)} %get-tuple-element.379, f32[]{:T(128)} %get-tuple-element.380), channel_id=1, replica_groups=mesh['lat'=4,'lon_0'=4,'lon_1'=8,'lon_2'=2] {'lon_1'}, use_global_device_ids=true, to_apply=%region_38.40 | all-reduce | flops 2 | bytes 16 | tf_op jit(solution)/shard_map/psum | solution.py:28
  339.2 10.9 %all-reduce.194 = (f32[]{:T(128)}, f32[]{:T(128)}) all-reduce(f32[]{:T(128)} %get-tuple-element.363, f32[]{:T(128)} %get-tuple-element.364), channel_id=1, replica_groups=mesh['lat'=4,'lon_0'=4,'lon_1'=8,'lon_2'=2] {'lon_2'}, use_global_device_ids=true, to_apply=%region_39.41 | all-reduce | flops 2 | bytes 16 | tf_op jit(solution)/shard_map/psum | solution.py:28
  375.5 9.2 %all-to-all-done.6 = f32[64,1,128]{2,1,0:T(1,128)S(1)} async-done(((f32[64,1,128]{2,1,0:T(1,128)}), f32[64,1,128]{2,1,0:T(1,128)S(1)}, u32[]{:S(2)}, u32[]{:S(2)}) %all-to-all-start.6) | async-done | bytes 32800 | tf_op jit(solution)/shard_map/all_to_all | solution.py:52
  400.6 11.6 %all-reduce.169 = (f32[]{:T(128)}, f32[]{:T(128)}) all-reduce(f32[]{:T(128)} %get-tuple-element.377, f32[]{:T(128)} %get-tuple-element.378), channel_id=1, replica_groups=mesh['lat'=4,'lon_0'=4,'lon_1'=8,'lon_2'=2] {'lon_1'}, use_global_device_ids=true, to_apply=%region_49.51 | all-reduce | flops 2 | bytes 16 | tf_op jit(solution)/shard_map/psum | solution.py:28
  412.3 11.0 %all-reduce.193 = (f32[]{:T(128)}, f32[]{:T(128)}) all-reduce(f32[]{:T(128)} %get-tuple-element.361, f32[]{:T(128)} %get-tuple-element.362), channel_id=1, replica_groups=mesh['lat'=4,'lon_0'=4,'lon_1'=8,'lon_2'=2] {'lon_2'}, use_global_device_ids=true, to_apply=%region_50.52 | all-reduce | flops 2 | bytes 16 | tf_op jit(solution)/shard_map/psum | solution.py:28
  448.6 9.2 %all-to-all-done.7 = f32[64,1,128]{2,1,0:T(1,128)S(1)} async-done(((f32[64,1,128]{2,1,0:T(1,128)}), f32[64,1,128]{2,1,0:T(1,128)S(1)}, u32[]{:S(2)}, u32[]{:S(2)}) %all-to-all-start.7) | async-done | bytes 32800 | tf_op jit(solution)/shard_map/all_to_all | solution.py:52
  473.9 11.7 %all-reduce.168 = (f32[]{:T(128)}, f32[]{:T(128)}) all-reduce(f32[]{:T(128)} %get-tuple-element.375, f32[]{:T(128)} %get-tuple-element.376), channel_id=1, replica_groups=mesh['lat'=4,'lon_0'=4,'lon_1'=8,'lon_2'=2] {'lon_1'}, use_global_device_ids=true, to_apply=%region_60.62 | all-reduce | flops 2 | bytes 16 | tf_op jit(solution)/shard_map/psum | solution.py:28
  485.6 11.2 %all-reduce.192 = (f32[]{:T(128)}, f32[]{:T(128)}) all-reduce(f32[]{:T(128)} %get-tuple-element.359, f32[]{:T(128)} %get-tuple-element.360), channel_id=1, replica_groups=mesh['lat'=4,'lon_0'=4,'lon_1'=8,'lon_2'=2] {'lon_2'}, use_global_device_ids=true, to_apply=%region_61.63 | all-reduce | flops 2 | bytes 16 | tf_op jit(solution)/shard_map/psum | solution.py:28
  522.1 9.2 %all-to-all-done.8 = f32[64,1,128]{2,1,0:T(1,128)S(1)} async-done(((f32[64,1,128]{2,1,0:T(1,128)}), f32[64,1,128]{2,1,0:T(1,128)S(1)}, u32[]{:S(2)}, u32[]{:S(2)}) %all-to-all-start.8) | async-done | bytes 32800 | tf_op jit(solution)/shard_map/all_to_all | solution.py:52
  547.3 11.6 %all-reduce.167 = (f32[]{:T(128)}, f32[]{:T(128)}) all-reduce(f32[]{:T(128)} %get-tuple-element.373, f32[]{:T(128)} %get-tuple-element.374), channel_id=1, replica_groups=mesh['lat'=4,'lon_0'=4,'lon_1'=8,'lon_2'=2] {'lon_1'}, use_global_device_ids=true, to_apply=%region_71.73 | all-reduce | flops 2 | bytes 16 | tf_op jit(solution)/shard_map/psum | solution.py:28
  558.9 11.0 %all-reduce.191 = (f32[]{:T(128)}, f32[]{:T(128)}) all-reduce(f32[]{:T(128)} %get-tuple-element.357, f32[]{:T(128)} %get-tuple-element.358), channel_id=1, replica_groups=mesh['lat'=4,'lon_0'=4,'lon_1'=8,'lon_2'=2] {'lon_2'}, use_global_device_ids=true, to_apply=%region_72.74 | all-reduce | flops 2 | bytes 16 | tf_op jit(solution)/shard_map/psum | solution.py:28
  595.3 9.2 %all-to-all-done.9 = f32[64,1,128]{2,1,0:T(1,128)S(1)} async-done(((f32[64,1,128]{2,1,0:T(1,128)}), f32[64,1,128]{2,1,0:T(1,128)S(1)}, u32[]{:S(2)}, u32[]{:S(2)}) %all-to-all-start.9) | async-done | bytes 32800 | tf_op jit(solution)/shard_map/all_to_all | solution.py:52
  620.5 11.7 %all-reduce.166 = (f32[]{:T(128)}, f32[]{:T(128)}) all-reduce(f32[]{:T(128)} %get-tuple-element.371, f32[]{:T(128)} %get-tuple-element.372), channel_id=1, replica_groups=mesh['lat'=4,'lon_0'=4,'lon_1'=8,'lon_2'=2] {'lon_1'}, use_global_device_ids=true, to_apply=%region_82.84 | all-reduce | flops 2 | bytes 16 | tf_op jit(solution)/shard_map/psum | solution.py:28
  632.2 11.0 %all-reduce.190 = (f32[]{:T(128)}, f32[]{:T(128)}) all-reduce(f32[]{:T(128)} %get-tuple-element.355, f32[]{:T(128)} %get-tuple-element.356), channel_id=1, replica_groups=mesh['lat'=4,'lon_0'=4,'lon_1'=8,'lon_2'=2] {'lon_2'}, use_global_device_ids=true, to_apply=%region_83.85 | all-reduce | flops 2 | bytes 16 | tf_op jit(solution)/shard_map/psum | solution.py:28
  (490 shorter events, 359.3 us)
Async XLA Ops:
  5.6 10.0 %collective-permute-start.1 = (f32[5,1,128]{1,2,0:T(8,128)S(1)}, f32[5,1,128]{1,2,0:T(8,128)S(1)}, u32[]{:S(2)}, u32[]{:S(2)}) collective-permute-start(f32[5,1,128]{1,2,0:T(8,128)S(1)} %get-tuple-element.486), channel_id=1, source_target_pairs={{64,0},{128,64},{192,128},{0,192},{65,1},{129,65},{193,129},{1,193... | collective-permute-start | bytes 7688 | tf_op jit(solution)/shard_map/ppermute | solution.py:39
  9.2 9.5 %collective-permute-start = (f32[5,1,128]{1,2,0:T(8,128)S(1)}, f32[5,1,128]{1,2,0:T(8,128)S(1)}, u32[]{:S(2)}, u32[]{:S(2)}) collective-permute-start(f32[5,1,128]{1,2,0:T(8,128)S(1)} %get-tuple-element.485), channel_id=1, source_target_pairs={{0,64},{64,128},{128,192},{192,0},{1,65},{65,129},{129,193},{193,1... | collective-permute-start | bytes 7688 | tf_op jit(solution)/shard_map/ppermute | solution.py:38
  34.5 11.4 %all-to-all-start = ((f32[4,4,128]{2,1,0:T(4,128)}), f32[4,4,128]{2,1,0:T(4,128)S(1)}, u32[]{:S(2)}, u32[]{:S(2)}) async-start(f32[4,4,128]{2,1,0:T(4,128)} %broadcast_in_dim.85), calls=%async_computation | async-start | bytes 16384 | tf_op jit(solution)/shard_map/all_to_all | solution.py:52
  50.9 21.4 %all-to-all-start.2 = ((f32[64,1,128]{2,1,0:T(1,128)}), f32[64,1,128]{2,1,0:T(1,128)S(1)}, u32[]{:S(2)}, u32[]{:S(2)}) async-start(f32[64,1,128]{2,1,0:T(1,128)} %broadcast_in_dim.94), calls=%async_computation.2 | async-start | bytes 65536 | tf_op jit(solution)/shard_map/all_to_all | solution.py:52
  63.1 14.9 %collective-permute-start.5 = (f32[130,1]{0,1:T(1,128)S(1)}, f32[130,1]{0,1:T(1,128)S(1)}, u32[]{:S(2)}, u32[]{:S(2)}) collective-permute-start(f32[130,1]{0,1:T(1,128)S(1)} %get-tuple-element.519), channel_id=1, source_target_pairs={{0,1},{1,2},{2,3},{3,4},{4,5},{5,6},{6,7},{7,8},{8,9},{9,10},{10,1... | collective-permute-start | bytes 1568 | tf_op jit(solution)/shard_map/ppermute | solution.py:38
  64.7 13.3 %collective-permute-start.4 = (f32[130,1]{0,1:T(1,128)S(1)}, f32[130,1]{0,1:T(1,128)S(1)}, u32[]{:S(2)}, u32[]{:S(2)}) collective-permute-start(f32[130,1]{0,1:T(1,128)S(1)} %get-tuple-element.520), channel_id=1, source_target_pairs={{1,0},{2,1},{3,2},{4,3},{5,4},{6,5},{7,6},{8,7},{9,8},{10,9},{11,1... | collective-permute-start | bytes 1568 | tf_op jit(solution)/shard_map/ppermute | solution.py:39
  72.9 14.7 %all-to-all-start.1 = ((f32[64,2,128]{2,1,0:T(2,128)}), f32[64,2,128]{2,1,0:T(2,128)S(1)}, u32[]{:S(2)}, u32[]{:S(2)}) async-start(f32[64,2,128]{2,1,0:T(2,128)} %broadcast_in_dim.91), calls=%async_computation.1 | async-start | bytes 131072 | tf_op jit(solution)/shard_map/all_to_all | solution.py:52
  142.1 12.3 %collective-permute-start.7 = (f32[130,1]{0,1:T(1,128)S(1)}, f32[130,1]{0,1:T(1,128)S(1)}, u32[]{:S(2)}, u32[]{:S(2)}) collective-permute-start(f32[130,1]{0,1:T(1,128)S(1)} %get-tuple-element.515), channel_id=1, source_target_pairs={{0,1},{1,2},{2,3},{3,4},{4,5},{5,6},{6,7},{7,8},{8,9},{9,10},{10,1... | collective-permute-start | bytes 1568 | tf_op jit(solution)/shard_map/ppermute | solution.py:38
  145.3 9.1 %collective-permute-start.6 = (f32[130,1]{0,1:T(1,128)S(1)}, f32[130,1]{0,1:T(1,128)S(1)}, u32[]{:S(2)}, u32[]{:S(2)}) collective-permute-start(f32[130,1]{0,1:T(1,128)S(1)} %get-tuple-element.516), channel_id=1, source_target_pairs={{1,0},{2,1},{3,2},{4,3},{5,4},{6,5},{7,6},{8,7},{9,8},{10,9},{11,1... | collective-permute-start | bytes 1568 | tf_op jit(solution)/shard_map/ppermute | solution.py:39
  146.2 17.6 %all-to-all-start.3 = ((f32[64,1,128]{2,1,0:T(1,128)}), f32[64,1,128]{2,1,0:T(1,128)S(1)}, u32[]{:S(2)}, u32[]{:S(2)}) async-start(f32[64,1,128]{2,1,0:T(1,128)} %broadcast_in_dim.95), calls=%async_computation.3 | async-start | bytes 65536 | tf_op jit(solution)/shard_map/all_to_all | solution.py:52
  216.3 12.3 %collective-permute-start.9 = (f32[130,1]{0,1:T(1,128)S(1)}, f32[130,1]{0,1:T(1,128)S(1)}, u32[]{:S(2)}, u32[]{:S(2)}) collective-permute-start(f32[130,1]{0,1:T(1,128)S(1)} %get-tuple-element.511), channel_id=1, source_target_pairs={{0,1},{1,2},{2,3},{3,4},{4,5},{5,6},{6,7},{7,8},{8,9},{9,10},{10,1... | collective-permute-start | bytes 1568 | tf_op jit(solution)/shard_map/ppermute | solution.py:38
  219.7 8.9 %collective-permute-start.8 = (f32[130,1]{0,1:T(1,128)S(1)}, f32[130,1]{0,1:T(1,128)S(1)}, u32[]{:S(2)}, u32[]{:S(2)}) collective-permute-start(f32[130,1]{0,1:T(1,128)S(1)} %get-tuple-element.512), channel_id=1, source_target_pairs={{1,0},{2,1},{3,2},{4,3},{5,4},{6,5},{7,6},{8,7},{9,8},{10,9},{11,1... | collective-permute-start | bytes 1568 | tf_op jit(solution)/shard_map/ppermute | solution.py:39
  220.5 17.5 %all-to-all-start.4 = ((f32[64,1,128]{2,1,0:T(1,128)}), f32[64,1,128]{2,1,0:T(1,128)S(1)}, u32[]{:S(2)}, u32[]{:S(2)}) async-start(f32[64,1,128]{2,1,0:T(1,128)} %broadcast_in_dim.96), calls=%async_computation.4 | async-start | bytes 65536 | tf_op jit(solution)/shard_map/all_to_all | solution.py:52
  289.5 12.5 %collective-permute-start.11 = (f32[130,1]{0,1:T(1,128)S(1)}, f32[130,1]{0,1:T(1,128)S(1)}, u32[]{:S(2)}, u32[]{:S(2)}) collective-permute-start(f32[130,1]{0,1:T(1,128)S(1)} %get-tuple-element.507), channel_id=1, source_target_pairs={{0,1},{1,2},{2,3},{3,4},{4,5},{5,6},{6,7},{7,8},{8,9},{9,10},{10,1... | collective-permute-start | bytes 1568 | tf_op jit(solution)/shard_map/ppermute | solution.py:38
  294.0 17.5 %all-to-all-start.5 = ((f32[64,1,128]{2,1,0:T(1,128)}), f32[64,1,128]{2,1,0:T(1,128)S(1)}, u32[]{:S(2)}, u32[]{:S(2)}) async-start(f32[64,1,128]{2,1,0:T(1,128)} %broadcast_in_dim.97), calls=%async_computation.5 | async-start | bytes 65536 | tf_op jit(solution)/shard_map/all_to_all | solution.py:52
  363.0 12.3 %collective-permute-start.13 = (f32[130,1]{0,1:T(1,128)S(1)}, f32[130,1]{0,1:T(1,128)S(1)}, u32[]{:S(2)}, u32[]{:S(2)}) collective-permute-start(f32[130,1]{0,1:T(1,128)S(1)} %get-tuple-element.503), channel_id=1, source_target_pairs={{0,1},{1,2},{2,3},{3,4},{4,5},{5,6},{6,7},{7,8},{8,9},{9,10},{10,1... | collective-permute-start | bytes 1568 | tf_op jit(solution)/shard_map/ppermute | solution.py:38
  367.2 17.5 %all-to-all-start.6 = ((f32[64,1,128]{2,1,0:T(1,128)}), f32[64,1,128]{2,1,0:T(1,128)S(1)}, u32[]{:S(2)}, u32[]{:S(2)}) async-start(f32[64,1,128]{2,1,0:T(1,128)} %broadcast_in_dim.98), calls=%async_computation.6 | async-start | bytes 65536 | tf_op jit(solution)/shard_map/all_to_all | solution.py:52
  436.1 12.3 %collective-permute-start.15 = (f32[130,1]{0,1:T(1,128)S(1)}, f32[130,1]{0,1:T(1,128)S(1)}, u32[]{:S(2)}, u32[]{:S(2)}) collective-permute-start(f32[130,1]{0,1:T(1,128)S(1)} %get-tuple-element.499), channel_id=1, source_target_pairs={{0,1},{1,2},{2,3},{3,4},{4,5},{5,6},{6,7},{7,8},{8,9},{9,10},{10,1... | collective-permute-start | bytes 1568 | tf_op jit(solution)/shard_map/ppermute | solution.py:38
  439.5 8.9 %collective-permute-start.14 = (f32[130,1]{0,1:T(1,128)S(1)}, f32[130,1]{0,1:T(1,128)S(1)}, u32[]{:S(2)}, u32[]{:S(2)}) collective-permute-start(f32[130,1]{0,1:T(1,128)S(1)} %get-tuple-element.500), channel_id=1, source_target_pairs={{1,0},{2,1},{3,2},{4,3},{5,4},{6,5},{7,6},{8,7},{9,8},{10,9},{11,1... | collective-permute-start | bytes 1568 | tf_op jit(solution)/shard_map/ppermute | solution.py:39
  440.3 17.5 %all-to-all-start.7 = ((f32[64,1,128]{2,1,0:T(1,128)}), f32[64,1,128]{2,1,0:T(1,128)S(1)}, u32[]{:S(2)}, u32[]{:S(2)}) async-start(f32[64,1,128]{2,1,0:T(1,128)} %broadcast_in_dim.99), calls=%async_computation.7 | async-start | bytes 65536 | tf_op jit(solution)/shard_map/all_to_all | solution.py:52
  509.6 12.3 %collective-permute-start.17 = (f32[130,1]{0,1:T(1,128)S(1)}, f32[130,1]{0,1:T(1,128)S(1)}, u32[]{:S(2)}, u32[]{:S(2)}) collective-permute-start(f32[130,1]{0,1:T(1,128)S(1)} %get-tuple-element.495), channel_id=1, source_target_pairs={{0,1},{1,2},{2,3},{3,4},{4,5},{5,6},{6,7},{7,8},{8,9},{9,10},{10,1... | collective-permute-start | bytes 1568 | tf_op jit(solution)/shard_map/ppermute | solution.py:38
  513.8 17.5 %all-to-all-start.8 = ((f32[64,1,128]{2,1,0:T(1,128)}), f32[64,1,128]{2,1,0:T(1,128)S(1)}, u32[]{:S(2)}, u32[]{:S(2)}) async-start(f32[64,1,128]{2,1,0:T(1,128)} %broadcast_in_dim.100), calls=%async_computation.8 | async-start | bytes 65536 | tf_op jit(solution)/shard_map/all_to_all | solution.py:52
  582.8 12.3 %collective-permute-start.19 = (f32[130,1]{0,1:T(1,128)S(1)}, f32[130,1]{0,1:T(1,128)S(1)}, u32[]{:S(2)}, u32[]{:S(2)}) collective-permute-start(f32[130,1]{0,1:T(1,128)S(1)} %get-tuple-element.491), channel_id=1, source_target_pairs={{0,1},{1,2},{2,3},{3,4},{4,5},{5,6},{6,7},{7,8},{8,9},{9,10},{10,1... | collective-permute-start | bytes 1568 | tf_op jit(solution)/shard_map/ppermute | solution.py:38
  587.0 17.5 %all-to-all-start.9 = ((f32[64,1,128]{2,1,0:T(1,128)}), f32[64,1,128]{2,1,0:T(1,128)S(1)}, u32[]{:S(2)}, u32[]{:S(2)}) async-start(f32[64,1,128]{2,1,0:T(1,128)} %broadcast_in_dim.101), calls=%async_computation.9 | async-start | bytes 65536 | tf_op jit(solution)/shard_map/all_to_all | solution.py:52
  (7 other events, 95.2 us)
where the time goes:
time: 659 us; the launch traced here: 649 us
  blocking collectives  350 us (53%)
  starting transfers between devices  110 us (17%)
  waiting for transfers between devices  86.9 us (13%)
  local copies, waits for them, and re-layouts  46.4 us (7%)
  between operations  32.6 us (5%)
  other arithmetic  23.6 us (4%)
    psum x32, blocking collectives, one_axis_at_a_time(): return functools.reduce(lax.psum, axes, shard)  293 us
    all_to_all x10, waiting for transfers between devices, copy_for_each(): return lax.all_to_all(copies, axis, split_axis=0, concat_axis=0, tiled=True)  80 us
    all_to_all x10, starting transfers between devices, copy_for_each(): return lax.all_to_all(copies, axis, split_axis=0, concat_axis=0, tiled=True)  77.1 us
    all_gather x8, blocking collectives, precondition(): gathered_ends = lax.all_gather(end_values, 'lat', axis=0, tiled=True)  56.5 us
    ppermute x10, starting transfers between devices, with_halo(): before = lax.ppermute(last, axis, up)  27 us
  transfers between devices with their start and end apart: 30, of which 12 were waited for; matrix products, arithmetic and copies ran while one was open for 3% of the time, Pallas kernels for 0%

commit v1 on v0

v1 whole, which is shorter than its diff:
```python
import functools

import jax
import jax.numpy as jnp
from jax import lax
from jax.experimental import pallas as pl
from jax.experimental.pallas import tpu as pltpu
from jax.sharding import Mesh
from jax.sharding import PartitionSpec as P

ITERS = 8
MESH = pl.DeviceIdType.MESH
LON = ("x", "z", "c")
F32 = jnp.float32


def roll(values, shift, axis):
    return pltpu.roll(values, shift % values.shape[axis], axis)


def halves(values):
    big = values * 4097.0
    high = big - (big - values)
    return high, values - high


def rounded_ratio(top, bottom):
    quotient = top / bottom
    q_high, q_low = halves(quotient)
    b_high, b_low = halves(bottom)
    product = quotient * bottom
    error = ((q_high * b_high - product) + q_high * b_low + q_low * b_high) + q_low * b_low
    return quotient + ((top - product) - error) / bottom


def start(src, dst, send_sem, recv_sem, device):
    pltpu.make_async_remote_copy(
        src_ref=src,
        dst_ref=dst,
        send_sem=send_sem,
        recv_sem=recv_sem,
        device_id=device,
        device_id_type=MESH,
    ).start()


def take(ref, sem):
    pltpu.make_async_copy(ref, ref, sem).wait()


def kernel(
    dims,
    rhs_ref, surf_ref, east_ref, north_ref, neast_ref, nwest_ref, land_ref, fold_ref,
    x_ref, r_ref,
    W, D, fac, invp, resp, g_ref, u, w, m, p, s, q, z, y, nf, vf,
    coef, fw, fmask, perm, me, ye, ge, dots, scal,
    e1s, e1r, e2s, e2r, e3s, e3r, c1s, c1r, c2r,
    hs, hr, s1s, s1r, fs, fr, a_s, a_r, ls, lr,
    e1sem, e2sem, e3sem, c1sem, c2sem, hsem, s1sem, fsem, asem, lsem,
):
    NL, NX, NZ, NC = dims
    NZC, NLX, NLON = NZ * NC, NL * NX, NX * NZ * NC
    n, cols = rhs_ref.shape
    lat, xx, zz, cc = (lax.axis_index(a) for a in ("lat",) + LON)
    zc = zz * NC + cc
    g2 = lat * NX + xx
    lon = xx * NZC + zc

    def lon_device(index):
        return (lat, index // NZC, (index // NC) % NZ, index % NC)

    east_dev = lon_device(lax.rem(lon + 1, NLON))
    west_dev = lon_device(lax.rem(lon + NLON - 1, NLON))
    zc_devs = []
    for d in range(1, NZC):
        t = lax.rem(zc + d, NZC)
        zc_devs.append((lat, xx, t // NC, t % NC))
    lx_devs = []
    for d in range(1, NLX):
        t = lax.rem(g2 + d, NLX)
        lx_devs.append((t // NX, t % NX, zz, cc))
    x_devs = [(lat, lax.rem(xx + d, NX), zz, cc) for d in range(1, NX)]
    lat_devs = [(lax.rem(lat + d, NL), xx, zz, cc) for d in range(1, NL)]

    barrier = pltpu.get_barrier_semaphore()
    greet = zc_devs + lx_devs + [east_dev, west_dev]
    for dev in greet:
        pl.semaphore_signal(barrier, inc=1, device_id=dev, device_id_type=MESH)

    row_ids = lax.broadcasted_iota(jnp.int32, (n, cols), 0)
    lane_ids = lax.broadcasted_iota(jnp.int32, (n, cols), 1)
    lane_row = lax.broadcasted_iota(jnp.int32, (1, cols), 1)
    is_top = jnp.where(lat == NL - 1, 1.0, 0.0).astype(F32)
    not_top = 1.0 - is_top
    not_bottom = jnp.where(lat == 0, 0.0, 1.0).astype(F32)
    top_at = jnp.where(lat == NL - 1, n - 1, -1)
    top_mask = row_ids == top_at

    def spread(vec):
        return jnp.transpose(jnp.broadcast_to(vec, (n, cols)))

    def from_west(field, vec):
        return jnp.where(lane_ids == 0, spread(vec), roll(field, 1, 1))

    def from_east(field, vec):
        return jnp.where(lane_ids == cols - 1, spread(vec), roll(field, cols - 1, 1))

    def row_from_west(row, other):
        return jnp.where(lane_row == 0, roll(other, 1, 1), roll(row, 1, 1))

    def row_from_east(row, other):
        return jnp.where(lane_row == cols - 1, roll(other, cols - 1, 1), roll(row, cols - 1, 1))

    def below(field, row):
        return jnp.where(row_ids == 0, row, roll(field, 1, 0))

    def above(field, row):
        return jnp.where(row_ids == n - 1, row, roll(field, n - 1, 0))

    def first(field):
        return field[0:1]

    def last(field):
        return field[n - 1 : n]

    levels = []
    stride = 1
    while stride < n:
        levels.append(stride)
        stride *= 2

    def local_solve(values):
        for i, stride in enumerate(levels):
            values = (
                values
                + fac[2 * i] * roll(values, stride, 0)
                + fac[2 * i + 1] * roll(values, n - stride, 0)
            )
        return values * invp[...]

    ocean = land_ref[...].astype(F32)
    raw_north = north_ref[...]
    east = east_ref[...]
    north = jnp.where(top_mask, 0.0, raw_north)
    neast = jnp.where(top_mask, 0.0, neast_ref[...])
    nwest = jnp.where(top_mask, 0.0, nwest_ref[...])
    rows1 = jnp.concatenate(
        [first(ocean), last(ocean), last(north), last(neast), last(nwest), last(raw_north)]
        + [last(ocean)] * 2,
        axis=0,
    )
    e1s[...] = rows1
    e1r[lat] = rows1
    residual = ocean * rhs_ref[...]
    r_ref[...] = residual
    x_ref[...] = jnp.zeros((n, cols), F32)
    for ref in (p, s, q, z, y):
        ref[...] = jnp.zeros((n, cols), F32)
    ye[...] = jnp.zeros(ye.shape, F32)
    dots[...] = jnp.zeros(dots.shape, F32)
    scal[...] = jnp.ones(scal.shape, F32)
    fold = fold_ref[...]
    fold0 = jnp.broadcast_to(fold[0:1, 0:1], (1, cols))
    offset = fold0 & (cols - 1)
    block_hi = fold0 // cols
    block_lo = jnp.where(block_hi == 0, NLON - 1, block_hi - 1)
    source_block = jnp.where(lane_row <= offset, block_hi, block_lo)
    lon_ids = lax.broadcasted_iota(jnp.int32, (NLON, cols), 0)
    fmask[...] = jnp.where(lon_ids == source_block, 1.0, 0.0)
    perm[...] = jnp.where(row_ids == (fold & (cols - 1)), 1.0, 0.0)

    def facing(row):
        return jnp.sum(spread(row) * perm[...], axis=0, keepdims=True)

    pl.semaphore_wait(barrier, len(greet))

    for dev in lat_devs:
        start(e1s, e1r.at[lat], e1sem.at[0], e1sem.at[1], dev)
    take(e1r.at[pl.ds(0, NL - 1)], e1sem.at[1])
    south_rows = e1r[jnp.maximum(lat - 1, 0)] * not_bottom
    north_rows = e1r[jnp.minimum(lat + 1, NL - 1)] * not_top
    top_rows = e1r[NL - 1]
    oc_s, n_s, ne_s, nw_s = (south_rows[i : i + 1] for i in range(1, 5))
    oc_n = north_rows[0:1]
    pair = jnp.concatenate([top_rows[5:6], top_rows[1:2]], axis=0)
    c1s[...] = pair
    c1r[zc] = pair
    for dev in zc_devs:
        start(c1s, c1r.at[zc], c1sem.at[0], c1sem.at[1], dev)

    oc_t, e_t, ne_t, nw_t = (jnp.transpose(f) for f in (ocean, east, neast, nwest))
    e2s[0] = jnp.concatenate(
        [last(oc_t), last(e_t), last(ne_t), oc_s, oc_n, ne_s, ne_s, ne_s], axis=0
    )
    e2s[1] = jnp.concatenate(
        [first(oc_t), first(nw_t), oc_s, oc_n, nw_s, nw_s, nw_s, nw_s], axis=0
    )
    start(e2s.at[0], e2r.at[0], e2sem.at[0], e2sem.at[1], east_dev)
    start(e2s.at[1], e2r.at[1], e2sem.at[2], e2sem.at[3], west_dev)

    surface = surf_ref[...]
    w_n = north * ocean * above(ocean, oc_n)
    w_s = below(north, n_s) * ocean * below(ocean, oc_s)
    W[2] = w_n
    W[3] = w_s
    middle = ocean * (surface + w_n + w_s) + (1.0 - ocean)
    lower = jnp.where(row_ids > 0, w_s, 0.0)
    upper = jnp.where(row_ids < n - 1, w_n, 0.0)
    excess = (middle - jnp.maximum(w_n, w_s)) - jnp.minimum(w_n, w_s)
    excess = excess + (w_s - lower) + (w_n - upper)
    start_middle = middle
    for i, stride in enumerate(levels):
        ratio = rounded_ratio if i == 0 else lax.div
        left = ratio(lower, roll(middle, stride, 0))
        right = ratio(upper, roll(middle, n - stride, 0))
        fac[2 * i] = left
        fac[2 * i + 1] = right
        pair_pivot = middle - roll(upper, stride, 0) * left - roll(lower, n - stride, 0) * right
        excess = excess + left * roll(excess, stride, 0) + right * roll(excess, n - stride, 0)
        lower = roll(lower, stride, 0) * left
        upper = roll(upper, n - stride, 0) * right
        if i == 0:
            beside = roll(pair_pivot, n - 1, 0) * (start_middle / roll(start_middle, n - 1, 0))
            pair_pivot = jnp.where(right > 0.0, beside, pair_pivot)
            coupled = lower + upper + jnp.minimum(left, right)
            excess = jnp.where(coupled == 0.0, pair_pivot, excess)
        middle = excess + lower + upper
    invp[...] = 1.0 / middle
    resp0 = local_solve(jnp.where(row_ids == 0, w_s, 0.0))
    resp1 = local_solve(jnp.where(row_ids == n - 1, w_n + jnp.where(top_mask, 1.0, 0.0), 0.0))
    resp[0] = resp0
    resp[1] = resp1
    local0 = local_solve(residual)
    rows3 = jnp.concatenate(
        [first(resp0), last(resp0), first(resp1), last(resp1), first(local0), last(local0)]
        + [last(local0)] * 2,
        axis=0,
    )
    e3s[...] = rows3
    e3r[lat] = rows3
    for dev in lat_devs:
        start(e3s, e3r.at[lat], e3sem.at[0], e3sem.at[1], dev)

    take(e2r.at[0], e2sem.at[1])
    take(e2r.at[1], e2sem.at[3])
    got_w = e2r[0]
    got_e = e2r[1]
    oc_w = from_west(ocean, got_w[0:1])
    e_w = from_west(east, got_w[1:2])
    ne_w = from_west(neast, got_w[2:3])
    oc_e = from_east(ocean, got_e[0:1])
    nw_e = from_east(nwest, got_e[1:2])
    oc_sw = row_from_west(oc_s, got_w[3:4])
    oc_nw = row_from_west(oc_n, got_w[4:5])
    ne_sw = row_from_west(ne_s, got_w[5:6])
    oc_se = row_from_east(oc_s, got_e[2:3])
    oc_ne = row_from_east(oc_n, got_e[3:4])
    nw_se = row_from_east(nw_s, got_e[4:5])
    n_down = below(north, n_s)
    ne_down = below(ne_w, ne_sw)
    nw_down = below(nw_e, nw_se)
    W[0] = east * ocean * oc_e
    W[1] = e_w * ocean * oc_w
    W[4] = neast * ocean * above(oc_e, oc_ne)
    W[5] = ne_down * ocean * below(oc_w, oc_sw)
    W[6] = nwest * ocean * above(oc_w, oc_nw)
    W[7] = nw_down * ocean * below(oc_e, oc_se)
    open_sum = east + e_w + north + n_down + neast + ne_down + nwest + nw_down
    D[...] = ocean * (surface + open_sum) + (1.0 - ocean)

    take(c1r.at[pl.ds(0, NZC - 1)], c1sem.at[1])
    c2r[xx] = c1r[...]
    for dev in x_devs:
        start(c1r, c2r.at[xx], c2sem.at[0], c2sem.at[1], dev)

    take(e3r.at[pl.ds(0, NL - 1)], e3sem.at[1])
    order = 2 * NL
    order_ids = lax.broadcasted_iota(jnp.int32, (order, cols), 0)
    ends = [e3r[b] for b in range(NL)]

    def unit(at):
        return jnp.where(order_ids == at, 1.0, 0.0)

    matrix, inverse = [], []
    for b in range(NL):
        for side in range(2):
            line = unit(2 * b + side)
            inverse.append(line)
            if b > 0:
                line = line - unit(2 * b - 1) * ends[b][side : side + 1]
            if b < NL - 1:
                line = line - unit(2 * b + 2) * ends[b][2 + side : 3 + side]
            matrix.append(line)
    for pivot in range(order):
        scale = 1.0 / matrix[pivot][pivot : pivot + 1]
        matrix[pivot] = matrix[pivot] * scale
        inverse[pivot] = inverse[pivot] * scale
        for i in range(order):
            if i != pivot:
                part = matrix[i][pivot : pivot + 1]
                matrix[i] = matrix[i] - part * matrix[pivot]
                inverse[i] = inverse[i] - part * inverse[pivot]
    coef_south = jnp.zeros((order, cols), F32)
    coef_north = jnp.zeros((order, cols), F32)
    for b in range(NL):
        here = jnp.where(lat == b, 1.0, 0.0).astype(F32)
        if b > 0:
            coef_south = coef_south + here * inverse[2 * b - 1]
        if b < NL - 1:
            coef_north = coef_north + here * inverse[2 * b + 2]
    coefs = (coef_south, coef_north, inverse[order - 1])
    for i, c in enumerate(coefs):
        for b in range(NL):
            coef[i, b] = c[2 * b : 2 * b + 2]

    def outer_rows(get):
        rows = []
        for i in range(3):
            total = coef[i, 0] * get(0)
            for b in range(1, NL):
                total = total + coef[i, b] * get(b)
            rows.append(jnp.sum(total, axis=0, keepdims=True))
        return rows

    def with_ends(local, rows):
        return local + rows[0] * resp[0] + rows[1] * resp[1]

    def stacked(rows):
        return jnp.concatenate(list(rows) + [rows[0]] * (8 - len(rows)), axis=0)

    rows = outer_rows(lambda b: e3r[b, 4:6])
    u0 = with_ends(local0, rows)
    u[...] = u0
    m[...] = u0
    me[...] = stacked(rows)
    g_ends = ends[NL - 1]
    g_rows = [
        c[order - 2 : order - 1] * g_ends[2:3] + c[order - 1 : order] * g_ends[3:4] for c in coefs
    ]
    g_ref[...] = is_top * resp1 + g_rows[0] * resp0 + g_rows[1] * resp1
    ge[...] = stacked(g_rows)

    if NX > 1:
        take(c2r.at[pl.ds(0, NX - 1)], c2sem.at[1])
    partner = jnp.zeros((2, cols), F32)
    for i in range(NX):
        for j in range(NZC):
            partner = partner + jnp.where(source_block == i * NZC + j, c2r[i, j], 0.0)
    fold_open = 0.5 * (top_rows[5:6] + facing(partner[0:1]))
    fw[...] = jnp.broadcast_to(fold_open * top_rows[1:2] * facing(partner[1:2]), fw.shape)
    D[...] = D[...] + jnp.where(top_mask, ocean * fold_open, 0.0)

    for ref, sem in (
        (e1r.at[pl.ds(0, NL - 1)], e1sem.at[0]),
        (c1r.at[pl.ds(0, NZC - 1)], c1sem.at[0]),
        (e2s.at[0], e2sem.at[0]),
        (e2s.at[1], e2sem.at[2]),
        (e3r.at[pl.ds(0, NL - 1)], e3sem.at[0]),
    ):
        take(ref, sem)
    if NX > 1:
        take(c2r.at[pl.ds(0, NX - 1)], c2sem.at[0])

    def send_stage1(par, top_row):
        mine = jnp.concatenate([top_row, dots[0:1], dots[1:2], dots[1:2]], axis=0)
        s1s[par] = mine
        s1r[par, zc] = mine
        for dev in zc_devs:
            start(s1s.at[par], s1r.at[par, zc], s1sem.at[0, par], s1sem.at[1, par], dev)

    def send_stage2(par, fold_too):
        take(s1r.at[par, pl.ds(0, NZC - 1)], s1sem.at[1, par])
        if fold_too:
            for j in range(NZC):
                row = s1r[par, j, 0:1]
                fs[par, j : j + 1] = row
                fr[par, xx, j : j + 1] = row
            for dev in x_devs:
                start(fs.at[par], fr.at[par, xx], fsem.at[0, par], fsem.at[1, par], dev)
        total = s1r[par, 0]
        for j in range(1, NZC):
            total = total + s1r[par, j]
        total = total[1:3]
        a_s[par] = total
        a_r[par, g2] = total
        for dev in lx_devs:
            start(a_s.at[par], a_r.at[par, g2], asem.at[0, par], asem.at[1, par], dev)

    def take_sums(par):
        take(a_r.at[par, pl.ds(0, NLX - 1)], asem.at[1, par])
        total = a_r[par, 0]
        for j in range(1, NLX):
            total = total + a_r[par, j]
        sums = jnp.broadcast_to(jnp.sum(total, axis=1, keepdims=True), (2, cols))
        return sums[0:1], sums[1:2]

    def sent(par, fold_too):
        take(s1r.at[par, pl.ds(0, NZC - 1)], s1sem.at[0, par])
        take(a_r.at[par, pl.ds(0, NLX - 1)], asem.at[0, par])
        if fold_too:
            if NX > 1:
                take(fr.at[par, pl.ds(0, NX - 1)], fsem.at[0, par])
            take(hs.at[par, 0], hsem.at[0, par])
            take(hs.at[par, 1], hsem.at[1, par])
            take(lr.at[par, pl.ds(0, NL - 1)], lsem.at[0, par])

    def step_sizes(gamma, delta, is_first):
        beta = jnp.where(is_first, 0.0, gamma / scal[0:1])
        alpha = gamma / (delta - beta * gamma / scal[1:2])
        return alpha, beta

    def set_dots():
        rr = r_ref[...]
        uu = u[...]
        dots[0:1] = jnp.sum(rr * uu, axis=0, keepdims=True)
        dots[1:2] = jnp.sum(w[...] * uu, axis=0, keepdims=True)

    def body(k, carry):
        par = lax.rem(k, 2)
        h = m[...]
        he = me[...]
        south, north_row = he[0:1], he[1:2]
        h_t = jnp.transpose(h)
        hs[par, 0] = jnp.concatenate([last(h_t), south, north_row, north_row], axis=0)
        hs[par, 1] = jnp.concatenate([first(h_t), south, north_row, north_row], axis=0)
        start(hs.at[par, 0], hr.at[par, 0], hsem.at[0, par], hsem.at[2, par], east_dev)
        start(hs.at[par, 1], hr.at[par, 1], hsem.at[1, par], hsem.at[3, par], west_dev)
        send_stage1(par, he[2:3])

        take(hr.at[par, 0], hsem.at[2, par])
        take(hr.at[par, 1], hsem.at[3, par])
        west = hr[par, 0]
        eastern = hr[par, 1]
        h_w = from_west(h, west[0:1])
        h_e = from_east(h, eastern[0:1])
        acc = D[...] * h - W[0] * h_e - W[1] * h_w
        acc = acc - W[2] * above(h, north_row) - W[3] * below(h, south)
        acc = acc - W[4] * above(h_e, row_from_east(north_row, eastern[2:3]))
        acc = acc - W[5] * below(h_w, row_from_west(south, west[1:2]))
        acc = acc - W[6] * above(h_w, row_from_west(north_row, west[2:3]))
        acc = acc - W[7] * below(h_e, row_from_east(south, eastern[1:2]))
        nf[...] = acc
        local = local_solve(acc)
        mine = jnp.concatenate([first(local), last(local)], axis=0)
        ls[par] = mine
        lr[par, lat] = mine
        for dev in lat_devs:
            start(ls.at[par], lr.at[par, lat], lsem.at[0, par], lsem.at[1, par], dev)

        send_stage2(par, True)

        take(lr.at[par, pl.ds(0, NL - 1)], lsem.at[1, par])
        rows = outer_rows(lambda b: lr[par, b])
        vf[...] = with_ends(local, rows)

        if NX > 1:
            take(fr.at[par, pl.ds(0, NX - 1)], fsem.at[1, par])
        picked = jnp.zeros((NZC, cols), F32)
        for i in range(NX):
            picked = picked + fmask[i * NZC : (i + 1) * NZC] * fr[par, i]
        f = fw[0:1] * facing(jnp.sum(picked, axis=0, keepdims=True))
        v = vf[...] - g_ref[...] * f
        ve = stacked(rows) - ge[...] * f
        nn = nf[...] - jnp.where(top_mask, f, 0.0)
        gamma, delta = take_sums(par)

        @pl.when(k == 0)
        def _():
            w[...] = nn
            m[...] = v
            me[...] = ve

        @pl.when(k > 0)
        def _():
            alpha, beta = step_sizes(gamma, delta, k == 1)
            scal[0:1] = gamma
            scal[1:2] = alpha
            y_new = v + beta * y[...]
            y[...] = y_new
            ye_new = ve + beta * ye[...]
            ye[...] = ye_new
            q_new = m[...] + beta * q[...]
            q[...] = q_new
            m[...] = m[...] - alpha * y_new
            me[...] = me[...] - alpha * ye_new
            s_new = w[...] + beta * s[...]
            s[...] = s_new
            z_new = nn + beta * z[...]
            z[...] = z_new
            w[...] = w[...] - alpha * z_new
            p_new = u[...] + beta * p[...]
            p[...] = p_new
            u[...] = u[...] - alpha * q_new
            x_ref[...] = x_ref[...] + alpha * p_new
            r_ref[...] = r_ref[...] - alpha * s_new

        set_dots()
        sent(par, True)
        return carry

    lax.fori_loop(0, ITERS, body, 0)

    par = ITERS % 2
    send_stage1(par, dots[0:1])
    send_stage2(par, False)
    gamma, delta = take_sums(par)
    alpha, beta = step_sizes(gamma, delta, False)
    x_ref[...] = x_ref[...] + alpha * (u[...] + beta * p[...])
    r_ref[...] = r_ref[...] - alpha * (w[...] + beta * s[...])
    sent(par, False)


def shards(dims, right_side, surface, east, north, neast, nwest, land_sea, fold_map):
    NL, NX, NZ, NC = dims
    NZC, NLX, NLON = NZ * NC, NL * NX, NX * NZ * NC
    n, cols = right_side.shape
    levels = (n - 1).bit_length()
    vmem = lambda *shape: pltpu.VMEM(shape, F32)
    field = lambda *lead: pltpu.VMEM(lead + (n, cols), F32)
    dma = pltpu.SemaphoreType.DMA
    scratch = [
        field(8), field(), field(2 * levels), field(), field(2), field(),
        *[field() for _ in range(8)],
        field(), field(),
        vmem(3, NL, 2, cols), vmem(8, cols), vmem(NLON, cols), field(),
        vmem(8, cols), vmem(8, cols), vmem(8, cols), vmem(8, cols), vmem(8, cols),
        vmem(8, cols), vmem(NL, 8, cols),
        vmem(2, 8, cols), vmem(2, 8, cols),
        vmem(8, cols), vmem(NL, 8, cols),
        vmem(2, cols), vmem(NZC, 2, cols), vmem(NX, NZC, 2, cols),
        vmem(2, 2, 4, cols), vmem(2, 2, 4, cols),
        vmem(2, 4, cols), vmem(2, NZC, 4, cols),
        vmem(2, NZC, cols), vmem(2, NX, NZC, cols),
        vmem(2, 2, cols), vmem(2, NLX, 2, cols),
        vmem(2, 2, cols), vmem(2, NL, 2, cols),
        dma((2,)), dma((4,)), dma((2,)), dma((2,)), dma((2,)),
        dma((4, 2)), dma((2, 2)), dma((2, 2)), dma((2, 2)), dma((2, 2)),
    ]
    spec = pl.BlockSpec(memory_space=pltpu.VMEM)
    shape = jax.ShapeDtypeStruct((n, cols), F32)
    return pl.pallas_call(
        functools.partial(kernel, dims),
        out_shape=(shape, shape),
        in_specs=[spec] * 8,
        out_specs=(spec, spec),
        scratch_shapes=scratch,
        compiler_params=pltpu.CompilerParams(collective_id=0, has_side_effects=True),
        name="pcg",
    )(right_side, surface, east, north, neast, nwest, land_sea, fold_map[None])


def build(devices, dims):
    finer = Mesh(devices.reshape(dims), ("lat",) + LON)
    both = P("lat", LON)
    return jax.shard_map(
        functools.partial(shards, dims),
        mesh=finer,
        in_specs=(both,) * 7 + (P(LON),),
        out_specs=(both, both),
        check_vma=False,
    )


def solution(mesh):
    return build(mesh.devices, (mesh.shape["lat"], 4, 8, 2))
```

time: 659 us -> 113 us (0.17); the launches traced: 649 us -> 113 us
  blocking collectives: 350 us -> 0 us
  Pallas kernels: 0 us -> 110 us
  starting transfers between devices: 110 us -> 0 us
  waiting for transfers between devices: 86.9 us -> 0 us
  local copies, waits for them, and re-layouts: 46.4 us -> 2.14 us
  between operations: 32.6 us -> 0.65 us
  other arithmetic: 23.6 us -> 0 us
    psum x32 -> x0, blocking collectives: 293 us -> none  [one_axis_at_a_time(): return functools.reduce(lax.psum, axes, shard)]
    pallas_call x0 -> x1, Pallas kernels: none -> 110 us  [shards(): pl.pallas_call(functools.partial(kernel, dims), out_shape=(shape, shape),...]
    all_to_all x10 -> x0, waiting for transfers between devices: 80 us -> none  [copy_for_each(): return lax.all_to_all(copies, axis, split_axis=0, concat_axis=0, tiled=True)]
    all_to_all x10 -> x0, starting transfers between devices: 77.1 us -> none  [copy_for_each(): return lax.all_to_all(copies, axis, split_axis=0, concat_axis=0, tiled=True)]
    all_gather x8 -> x0, blocking collectives: 56.5 us -> none  [precondition(): gathered_ends = lax.all_gather(end_values, 'lat', axis=0, tiled=True)]
    ppermute x20 -> x0, starting transfers between devices: 32.5 us -> none  [the longest x10 27 us: with_halo(): before = lax.ppermute(last, axis, up)]
    gather x9 -> x0, local copies, waits for them, and re-layouts: 12 us -> none  [the longest x8 9.18 us: operate(): fold_term = fold_weight * jnp.take(whole_row, fold_map)]
    slice x128 -> x0, local copies, waits for them, and re-layouts: 11.1 us -> none  [the longest x67 5.41 us: shift_down(): return jnp.concatenate([filler, values[..., :-stride, :]], axis=-2)]
  transfers between devices with their start and end apart: 30 -> 0, of which waited for: 12 -> 0; matrix products, arithmetic and copies ran while one was open for 3% -> 0% of each run, Pallas kernels for 0% -> 0%
where the time goes in v1:
time: 113 us
  Pallas kernels  110 us (97%)
  local copies, waits for them, and re-layouts  2.14 us (2%)
    pallas_call x1, Pallas kernels, shards(): pl.pallas_call(functools.partial(kernel, dims), out_shape=(shape, shape),...  110 us

profile of v1, /device:TPU:1, one launch (start us, length us, event | category | flops | bytes accessed | tf_op | source)
XLA Modules:
  0.0 113.3 jit_solution(9470339989901841964)
XLA Ops:
  0.6 110.5 %pcg.1 = (f32[128,128]{1,0:T(8,128)}, f32[128,128]{1,0:T(8,128)}) custom-call(f32[128,128]{1,0:T(8,128)} %rhs_ref.1, f32[128,128]{1,0:T(8,128)} %surf_ref.1, f32[128,128]{1,0:T(8,128)} %east_ref.1, f32[128,128]{1,0:T(8,128)} %north_ref.1, f32[128,128]{1,0:T(8,128)} %neast_ref.1, f32[128,128]{1,0:T(8,128)} %nwest_ref.1, s32[128,128]{1,0:T(8,128)} %land_ref.1, ...), custom_call_target="tpu_custom_call" | custom-call | tf_op jit(solution)/shard_map/pcg/pallas_call | solution.py:541
  111.1 0.0 copy-start
  111.1 1.5 %copy.12 = f32[128,128]{1,0:T(8,128)} copy(f32[128,128]{1,0:T(8,128)} %get-tuple-element.4) | data formatting | bytes 131072
  112.6 0.0 copy-done
  112.6 0.6 copy.13
Async XLA Ops:
  111.1 1.5 %copy-start = (f32[128,128]{1,0:T(8,128)S(1)}, f32[128,128]{1,0:T(8,128)}, u32[]{:S(2)}) copy-start(f32[128,128]{1,0:T(8,128)} %get-tuple-element.5) | copy-start | bytes 196612

commit v2 on v1

--- a/solution.py
+++ b/solution.py
@@ -9,6 +9,7 @@
 from jax.sharding import PartitionSpec as P
 
 ITERS = 8
+SHORT = 6
 MESH = pl.DeviceIdType.MESH
 LON = ("x", "z", "c")
 F32 = jnp.float32
@@ -203,29 +204,32 @@
     w_s = below(north, n_s) * ocean * below(ocean, oc_s)
     W[2] = w_n
     W[3] = w_s
-    middle = ocean * (surface + w_n + w_s) + (1.0 - ocean)
+    diagonal = ocean * (surface + w_n + w_s) + (1.0 - ocean)
     lower = jnp.where(row_ids > 0, w_s, 0.0)
     upper = jnp.where(row_ids < n - 1, w_n, 0.0)
-    excess = (middle - jnp.maximum(w_n, w_s)) - jnp.minimum(w_n, w_s)
+    excess = (diagonal - jnp.maximum(w_n, w_s)) - jnp.minimum(w_n, w_s)
     excess = excess + (w_s - lower) + (w_n - upper)
-    start_middle = middle
+    plain, kept = diagonal, excess
+    whole = jnp.where(w_s == 0.0, 1.0, 0.0)
+    begins = whole
+    for _ in range(SHORT - 1):
+        plain = diagonal - lower * rounded_ratio(lower, roll(plain, 1, 0))
+        kept = excess + lower / roll(kept + upper, 1, 0) * roll(kept, 1, 0)
+        whole = jnp.where(lower > 0.0, roll(whole, 1, 0), begins)
+    ratio = jnp.where((w_n == 0.0) & (whole > 0.0), kept / plain, 1.0)
+    for _ in range(SHORT - 1):
+        ratio = jnp.where(upper > 0.0, roll(ratio, n - 1, 0), ratio)
+    middle = excess + lower + upper
     for i, stride in enumerate(levels):
-        ratio = rounded_ratio if i == 0 else lax.div
-        left = ratio(lower, roll(middle, stride, 0))
-        right = ratio(upper, roll(middle, n - stride, 0))
+        left = lower / roll(middle, stride, 0)
+        right = upper / roll(middle, n - stride, 0)
         fac[2 * i] = left
         fac[2 * i + 1] = right
-        pair_pivot = middle - roll(upper, stride, 0) * left - roll(lower, n - stride, 0) * right
         excess = excess + left * roll(excess, stride, 0) + right * roll(excess, n - stride, 0)
         lower = roll(lower, stride, 0) * left
         upper = roll(upper, n - stride, 0) * right
-        if i == 0:
-            beside = roll(pair_pivot, n - 1, 0) * (start_middle / roll(start_middle, n - 1, 0))
-            pair_pivot = jnp.where(right > 0.0, beside, pair_pivot)
-            coupled = lower + upper + jnp.minimum(left, right)
-            excess = jnp.where(coupled == 0.0, pair_pivot, excess)
         middle = excess + lower + upper
-    invp[...] = 1.0 / middle
+    invp[...] = ratio / middle
     resp0 = local_solve(jnp.where(row_ids == 0, w_s, 0.0))
     resp1 = local_solve(jnp.where(row_ids == n - 1, w_n + jnp.where(top_mask, 1.0, 0.0), 0.0))
     resp[0] = resp0

time: 113 us -> 113 us (level)
  no operation moved by 1% of the time
where the time goes in v2:
time: 113 us
  Pallas kernels  110 us (97%)
  local copies, waits for them, and re-layouts  2.14 us (2%)
    pallas_call x1, Pallas kernels, shards(): pl.pallas_call(functools.partial(kernel, dims), out_shape=(shape, shape),...  110 us

profile of v2, /device:TPU:1, one launch (start us, length us, event | category | flops | bytes accessed | tf_op | source)
XLA Modules:
  0.0 113.3 jit_solution(12516662428729097212)
XLA Ops:
  0.6 110.5 %pcg.1 = (f32[128,128]{1,0:T(8,128)}, f32[128,128]{1,0:T(8,128)}) custom-call(f32[128,128]{1,0:T(8,128)} %rhs_ref.1, f32[128,128]{1,0:T(8,128)} %surf_ref.1, f32[128,128]{1,0:T(8,128)} %east_ref.1, f32[128,128]{1,0:T(8,128)} %north_ref.1, f32[128,128]{1,0:T(8,128)} %neast_ref.1, f32[128,128]{1,0:T(8,128)} %nwest_ref.1, s32[128,128]{1,0:T(8,128)} %land_ref.1, ...), custom_call_target="tpu_custom_call" | custom-call | tf_op jit(solution)/shard_map/pcg/pallas_call | solution.py:545
  111.1 0.0 copy-start
  111.1 1.5 %copy.12 = f32[128,128]{1,0:T(8,128)} copy(f32[128,128]{1,0:T(8,128)} %get-tuple-element.4) | data formatting | bytes 131072
  112.6 0.0 copy-done
  112.6 0.6 copy.13
Async XLA Ops:
  111.1 1.5 %copy-start = (f32[128,128]{1,0:T(8,128)S(1)}, f32[128,128]{1,0:T(8,128)}, u32[]{:S(2)}) copy-start(f32[128,128]{1,0:T(8,128)} %get-tuple-element.5) | copy-start | bytes 196612

commit v3 on v2

--- a/solution.py
+++ b/solution.py
@@ -54,37 +54,26 @@
     rhs_ref, surf_ref, east_ref, north_ref, neast_ref, nwest_ref, land_ref, fold_ref,
     x_ref, r_ref,
     W, D, fac, invp, resp, g_ref, u, w, m, p, s, q, z, y, nf, vf,
-    coef, fw, fmask, perm, me, ye, ge, dots, scal,
-    e1s, e1r, e2s, e2r, e3s, e3r, c1s, c1r, c2r,
-    hs, hr, s1s, s1r, fs, fr, a_s, a_r, ls, lr,
-    e1sem, e2sem, e3sem, c1sem, c2sem, hsem, s1sem, fsem, asem, lsem,
+    coef, fw, perm, me, ye, ge, dots, scal,
+    e1s, e1r, e2s, e2r, e3s, e3r, cs, cr, hs, hr, gs, gr, ls, lr,
+    e1sem, e2sem, e3sem, csem, hsem, gsem, lsem,
 ):
     NL, NX, NZ, NC = dims
-    NZC, NLX, NLON = NZ * NC, NL * NX, NX * NZ * NC
+    NZC, NLON = NZ * NC, NX * NZ * NC
     n, cols = rhs_ref.shape
     lat, xx, zz, cc = (lax.axis_index(a) for a in ("lat",) + LON)
-    zc = zz * NC + cc
-    g2 = lat * NX + xx
-    lon = xx * NZC + zc
+    lon = xx * NZC + zz * NC + cc
 
     def lon_device(index):
         return (lat, index // NZC, (index // NC) % NZ, index % NC)
 
     east_dev = lon_device(lax.rem(lon + 1, NLON))
     west_dev = lon_device(lax.rem(lon + NLON - 1, NLON))
-    zc_devs = []
-    for d in range(1, NZC):
-        t = lax.rem(zc + d, NZC)
-        zc_devs.append((lat, xx, t // NC, t % NC))
-    lx_devs = []
-    for d in range(1, NLX):
-        t = lax.rem(g2 + d, NLX)
-        lx_devs.append((t // NX, t % NX, zz, cc))
-    x_devs = [(lat, lax.rem(xx + d, NX), zz, cc) for d in range(1, NX)]
+    plane_devs = [lon_device(lax.rem(lon + d, NLON)) for d in range(1, NLON)]
     lat_devs = [(lax.rem(lat + d, NL), xx, zz, cc) for d in range(1, NL)]
 
     barrier = pltpu.get_barrier_semaphore()
-    greet = zc_devs + lx_devs + [east_dev, west_dev]
+    greet = plane_devs + lat_devs
     for dev in greet:
         pl.semaphore_signal(barrier, inc=1, device_id=dev, device_id_type=MESH)
 
@@ -166,8 +155,6 @@
     block_hi = fold0 // cols
     block_lo = jnp.where(block_hi == 0, NLON - 1, block_hi - 1)
     source_block = jnp.where(lane_row <= offset, block_hi, block_lo)
-    lon_ids = lax.broadcasted_iota(jnp.int32, (NLON, cols), 0)
-    fmask[...] = jnp.where(lon_ids == source_block, 1.0, 0.0)
     perm[...] = jnp.where(row_ids == (fold & (cols - 1)), 1.0, 0.0)
 
     def facing(row):
@@ -184,10 +171,10 @@
     oc_s, n_s, ne_s, nw_s = (south_rows[i : i + 1] for i in range(1, 5))
     oc_n = north_rows[0:1]
     pair = jnp.concatenate([top_rows[5:6], top_rows[1:2]], axis=0)
-    c1s[...] = pair
-    c1r[zc] = pair
-    for dev in zc_devs:
-        start(c1s, c1r.at[zc], c1sem.at[0], c1sem.at[1], dev)
+    cs[...] = pair
+    cr[lon] = pair
+    for dev in plane_devs:
+        start(cs, cr.at[lon], csem.at[0], csem.at[1], dev)
 
     oc_t, e_t, ne_t, nw_t = (jnp.transpose(f) for f in (ocean, east, neast, nwest))
     e2s[0] = jnp.concatenate(
@@ -272,11 +259,6 @@
     open_sum = east + e_w + north + n_down + neast + ne_down + nwest + nw_down
     D[...] = ocean * (surface + open_sum) + (1.0 - ocean)
 
-    take(c1r.at[pl.ds(0, NZC - 1)], c1sem.at[1])
-    c2r[xx] = c1r[...]
-    for dev in x_devs:
-        start(c1r, c2r.at[xx], c2sem.at[0], c2sem.at[1], dev)
-
     take(e3r.at[pl.ds(0, NL - 1)], e3sem.at[1])
     order = 2 * NL
     order_ids = lax.broadcasted_iota(jnp.int32, (order, cols), 0)
@@ -344,80 +326,53 @@
     g_ref[...] = is_top * resp1 + g_rows[0] * resp0 + g_rows[1] * resp1
     ge[...] = stacked(g_rows)
 
-    if NX > 1:
-        take(c2r.at[pl.ds(0, NX - 1)], c2sem.at[1])
+    take(cr.at[pl.ds(0, NLON - 1)], csem.at[1])
     partner = jnp.zeros((2, cols), F32)
-    for i in range(NX):
-        for j in range(NZC):
-            partner = partner + jnp.where(source_block == i * NZC + j, c2r[i, j], 0.0)
+    for j in range(NLON):
+        partner = partner + jnp.where(source_block == j, cr[j], 0.0)
     fold_open = 0.5 * (top_rows[5:6] + facing(partner[0:1]))
     fw[...] = jnp.broadcast_to(fold_open * top_rows[1:2] * facing(partner[1:2]), fw.shape)
     D[...] = D[...] + jnp.where(top_mask, ocean * fold_open, 0.0)
 
     for ref, sem in (
         (e1r.at[pl.ds(0, NL - 1)], e1sem.at[0]),
-        (c1r.at[pl.ds(0, NZC - 1)], c1sem.at[0]),
+        (cr.at[pl.ds(0, NLON - 1)], csem.at[0]),
         (e2s.at[0], e2sem.at[0]),
         (e2s.at[1], e2sem.at[2]),
         (e3r.at[pl.ds(0, NL - 1)], e3sem.at[0]),
     ):
         take(ref, sem)
-    if NX > 1:
-        take(c2r.at[pl.ds(0, NX - 1)], c2sem.at[0])
-
-    def send_stage1(par, top_row):
-        mine = jnp.concatenate([top_row, dots[0:1], dots[1:2], dots[1:2]], axis=0)
-        s1s[par] = mine
-        s1r[par, zc] = mine
-        for dev in zc_devs:
-            start(s1s.at[par], s1r.at[par, zc], s1sem.at[0, par], s1sem.at[1, par], dev)
-
-    def send_stage2(par, fold_too):
-        take(s1r.at[par, pl.ds(0, NZC - 1)], s1sem.at[1, par])
-        if fold_too:
-            for j in range(NZC):
-                row = s1r[par, j, 0:1]
-                fs[par, j : j + 1] = row
-                fr[par, xx, j : j + 1] = row
-            for dev in x_devs:
-                start(fs.at[par], fr.at[par, xx], fsem.at[0, par], fsem.at[1, par], dev)
-        total = s1r[par, 0]
-        for j in range(1, NZC):
-            total = total + s1r[par, j]
-        total = total[1:3]
-        a_s[par] = total
-        a_r[par, g2] = total
-        for dev in lx_devs:
-            start(a_s.at[par], a_r.at[par, g2], asem.at[0, par], asem.at[1, par], dev)
-
-    def take_sums(par):
-        take(a_r.at[par, pl.ds(0, NLX - 1)], asem.at[1, par])
-        total = a_r[par, 0]
-        for j in range(1, NLX):
-            total = total + a_r[par, j]
-        sums = jnp.broadcast_to(jnp.sum(total, axis=1, keepdims=True), (2, cols))
-        return sums[0:1], sums[1:2]
-
-    def sent(par, fold_too):
-        take(s1r.at[par, pl.ds(0, NZC - 1)], s1sem.at[0, par])
-        take(a_r.at[par, pl.ds(0, NLX - 1)], asem.at[0, par])
-        if fold_too:
-            if NX > 1:
-                take(fr.at[par, pl.ds(0, NX - 1)], fsem.at[0, par])
-            take(hs.at[par, 0], hsem.at[0, par])
-            take(hs.at[par, 1], hsem.at[1, par])
-            take(lr.at[par, pl.ds(0, NL - 1)], lsem.at[0, par])
-
-    def step_sizes(gamma, delta, is_first):
-        beta = jnp.where(is_first, 0.0, gamma / scal[0:1])
-        alpha = gamma / (delta - beta * gamma / scal[1:2])
-        return alpha, beta
-
-    def set_dots():
-        rr = r_ref[...]
-        uu = u[...]
-        dots[0:1] = jnp.sum(rr * uu, axis=0, keepdims=True)
-        dots[1:2] = jnp.sum(w[...] * uu, axis=0, keepdims=True)
+
+    def gather_top(par, top_row):
+        mine = jnp.concatenate([top_row, dots[0:1]], axis=0)
+        gs[par] = mine
+        gr[par, lon] = mine
+        for dev in plane_devs:
+            start(gs.at[par], gr.at[par, lon], gsem.at[0, par], gsem.at[1, par], dev)
+
+    def total(field):
+        return jnp.sum(field, axis=(0, 1), keepdims=True)
+
+    def packed(sums):
+        row = jnp.zeros((1, cols), F32)
+        for at, value in sums.items():
+            row = jnp.where(lane_row == at, value, row)
+        return row
+
+    def step_sizes(row, is_first):
+        g0, g1, d2, d3, d4, d5, d6, d7, d8 = (
+            jnp.broadcast_to(row[0:1, j : j + 1], (1, cols)) for j in range(9)
+        )
+        alpha, beta = scal[0:1], scal[1:2]
+        qu = g1 + beta * d2
+        qq = d3 + 2.0 * beta * d4 + beta * beta * d5
+        qm = d3 + beta * d4
+        qy = d6 + 2.0 * beta * d7 + beta * beta * d8
+        gamma = g0 - 2.0 * alpha * qu + alpha * alpha * qq
+        delta = g1 - 2.0 * alpha * qm + alpha * alpha * qy
+        beta_next = gamma / g0
+        alpha_next = gamma / (delta - beta_next * gamma / alpha)
+        return jnp.where(is_first, g0 / d6, alpha_next), jnp.where(is_first, 0.0, beta_next)
 
     def body(k, carry):
         par = lax.rem(k, 2)
@@ -429,8 +384,13 @@
         hs[par, 1] = jnp.concatenate([first(h_t), south, north_row, north_row], axis=0)
         start(hs.at[par, 0], hr.at[par, 0], hsem.at[0, par], hsem.at[2, par], east_dev)
         start(hs.at[par, 1], hr.at[par, 1], hsem.at[1, par], hsem.at[3, par], west_dev)
-        send_stage1(par, he[2:3])
-
+        gather_top(par, he[2:3])
+
+        rr, uu, ww, ss, qq, zz_ = r_ref[...], u[...], w[...], s[...], q[...], z[...]
+        sums = {
+            0: total(rr * uu), 1: total(ww * uu), 2: total(ss * uu), 3: total(ww * h), 4: total(ss * h),
+            5: total(ss * qq), 7: total(zz_ * h), 8: total(zz_ * qq),
+        }
         take(hr.at[par, 0], hsem.at[2, par])
         take(hr.at[par, 1], hsem.at[3, par])
         west = hr[par, 0]
@@ -445,28 +405,35 @@
         acc = acc - W[7] * below(h_e, row_from_east(south, eastern[1:2]))
         nf[...] = acc
         local = local_solve(acc)
-        mine = jnp.concatenate([first(local), last(local)], axis=0)
+        sums[6] = total(acc * h)
+        sums_row = packed(sums)
+        mine = jnp.concatenate([first(local), last(local), sums_row, sums_row], axis=0)
         ls[par] = mine
         lr[par, lat] = mine
         for dev in lat_devs:
             start(ls.at[par], lr.at[par, lat], lsem.at[0, par], lsem.at[1, par], dev)
 
-        send_stage2(par, True)
-
         take(lr.at[par, pl.ds(0, NL - 1)], lsem.at[1, par])
-        rows = outer_rows(lambda b: lr[par, b])
+        rows = outer_rows(lambda b: lr[par, b, 0:2])
+        sums_row = lr[par, 0, 2:3]
+        for b in range(1, NL):
+            sums_row = sums_row + lr[par, b, 2:3]
         vf[...] = with_ends(local, rows)
 
-        if NX > 1:
-            take(fr.at[par, pl.ds(0, NX - 1)], fsem.at[1, par])
-        picked = jnp.zeros((NZC, cols), F32)
-        for i in range(NX):
-            picked = picked + fmask[i * NZC : (i + 1) * NZC] * fr[par, i]
-        f = fw[0:1] * facing(jnp.sum(picked, axis=0, keepdims=True))
+        take(gr.at[par, pl.ds(0, NLON - 1)], gsem.at[1, par])
+        picked = [jnp.zeros((2, cols), F32) for _ in range(4)]
+        summed = [jnp.zeros((2, cols), F32) for _ in range(4)]
+        for j in range(NLON):
+            got = gr[par, j]
+            picked[j % 4] = picked[j % 4] + jnp.where(source_block == j, got, 0.0)
+            summed[j % 4] = summed[j % 4] + got
+        row = ((picked[0] + picked[1]) + (picked[2] + picked[3]))[0:1]
+        whole_sums = ((summed[0] + summed[1]) + (summed[2] + summed[3]))[1:2]
+        f = fw[0:1] * facing(row)
+        dots[0:1] = sums_row - jnp.where(lane_row == 6, total(f * he[2:3]), 0.0)
         v = vf[...] - g_ref[...] * f
         ve = stacked(rows) - ge[...] * f
         nn = nf[...] - jnp.where(top_mask, f, 0.0)
-        gamma, delta = take_sums(par)
 
         @pl.when(k == 0)
         def _():
@@ -476,9 +443,9 @@
 
         @pl.when(k > 0)
         def _():
-            alpha, beta = step_sizes(gamma, delta, k == 1)
-            scal[0:1] = gamma
-            scal[1:2] = alpha
+            alpha, beta = step_sizes(whole_sums, k == 1)
+            scal[0:1] = alpha
+            scal[1:2] = beta
             y_new = v + beta * y[...]
             y[...] = y_new
             ye_new = ve + beta * ye[...]
@@ -498,25 +465,29 @@
             x_ref[...] = x_ref[...] + alpha * p_new
             r_ref[...] = r_ref[...] - alpha * s_new
 
-        set_dots()
-        sent(par, True)
+        take(hs.at[par, 0], hsem.at[0, par])
+        take(hs.at[par, 1], hsem.at[1, par])
+        take(gr.at[par, pl.ds(0, NLON - 1)], gsem.at[0, par])
+        take(lr.at[par, pl.ds(0, NL - 1)], lsem.at[0, par])
         return carry
 
     lax.fori_loop(0, ITERS, body, 0)
 
     par = ITERS % 2
-    send_stage1(par, dots[0:1])
-    send_stage2(par, False)
-    gamma, delta = take_sums(par)
-    alpha, beta = step_sizes(gamma, delta, False)
+    gather_top(par, dots[0:1])
+    take(gr.at[par, pl.ds(0, NLON - 1)], gsem.at[1, par])
+    summed = [jnp.zeros((2, cols), F32) for _ in range(4)]
+    for j in range(NLON):
+        summed[j % 4] = summed[j % 4] + gr[par, j]
+    alpha, beta = step_sizes(((summed[0] + summed[1]) + (summed[2] + summed[3]))[1:2], False)
     x_ref[...] = x_ref[...] + alpha * (u[...] + beta * p[...])
     r_ref[...] = r_ref[...] - alpha * (w[...] + beta * s[...])
-    sent(par, False)
+    take(gr.at[par, pl.ds(0, NLON - 1)], gsem.at[0, par])
 
 
 def shards(dims, right_side, surface, east, north, neast, nwest, land_sea, fold_map):
     NL, NX, NZ, NC = dims
-    NZC, NLX, NLON = NZ * NC, NL * NX, NX * NZ * NC
+    NLON = NX * NZ * NC
     n, cols = right_side.shape
     levels = (n - 1).bit_length()
     vmem = lambda *shape: pltpu.VMEM(shape, F32)
@@ -526,19 +497,17 @@
         field(8), field(), field(2 * levels), field(), field(2), field(),
         *[field() for _ in range(8)],
         field(), field(),
-        vmem(3, NL, 2, cols), vmem(8, cols), vmem(NLON, cols), field(),
+        vmem(3, NL, 2, cols), vmem(8, cols), field(),
         vmem(8, cols), vmem(8, cols), vmem(8, cols), vmem(8, cols), vmem(8, cols),
         vmem(8, cols), vmem(NL, 8, cols),
         vmem(2, 8, cols), vmem(2, 8, cols),
         vmem(8, cols), vmem(NL, 8, cols),
-        vmem(2, cols), vmem(NZC, 2, cols), vmem(NX, NZC, 2, cols),
+        vmem(2, cols), vmem(NLON, 2, cols),
         vmem(2, 2, 4, cols), vmem(2, 2, 4, cols),
-        vmem(2, 4, cols), vmem(2, NZC, 4, cols),
-        vmem(2, NZC, cols), vmem(2, NX, NZC, cols),
-        vmem(2, 2, cols), vmem(2, NLX, 2, cols),
-        vmem(2, 2, cols), vmem(2, NL, 2, cols),
-        dma((2,)), dma((4,)), dma((2,)), dma((2,)), dma((2,)),
-        dma((4, 2)), dma((2, 2)), dma((2, 2)), dma((2, 2)), dma((2, 2)),
+        vmem(2, 2, cols), vmem(2, NLON, 2, cols),
+        vmem(2, 4, cols), vmem(2, NL, 4, cols),
+        dma((2,)), dma((4,)), dma((2,)), dma((2,)),
+        dma((4, 2)), dma((2, 2)), dma((2, 2)),
     ]
     spec = pl.BlockSpec(memory_space=pltpu.VMEM)
     shape = jax.ShapeDtypeStruct((n, cols), F32)

time: 113 us -> 94.6 us (0.84)
  Pallas kernels: 110 us -> 91.7 us
    pallas_call x1, Pallas kernels: 110 us -> 91.7 us  [shards(): pl.pallas_call(functools.partial(kernel, dims), out_shape=(shape, shape),...]
where the time goes in v3:
time: 94.6 us; the launch traced here: 94.5 us
  Pallas kernels  91.7 us (97%)
  local copies, waits for them, and re-layouts  2.14 us (2%)
    pallas_call x1, Pallas kernels, shards(): pl.pallas_call(functools.partial(kernel, dims), out_shape=(shape, shape),...  91.7 us
    unnamed x4, local copies, waits for them, and re-layouts  2.14 us

profile of v3, /device:TPU:1, one launch (start us, length us, event | category | flops | bytes accessed | tf_op | source)
XLA Modules:
  0.0 94.5 jit_solution(3453534402601680480)
XLA Ops:
  0.6 91.7 %pcg.1 = (f32[128,128]{1,0:T(8,128)}, f32[128,128]{1,0:T(8,128)}) custom-call(f32[128,128]{1,0:T(8,128)} %rhs_ref.1, f32[128,128]{1,0:T(8,128)} %surf_ref.1, f32[128,128]{1,0:T(8,128)} %east_ref.1, f32[128,128]{1,0:T(8,128)} %north_ref.1, f32[128,128]{1,0:T(8,128)} %neast_ref.1, f32[128,128]{1,0:T(8,128)} %nwest_ref.1, s32[128,128]{1,0:T(8,128)} %land_ref.1, ...), custom_call_target="tpu_custom_call" | custom-call | tf_op jit(solution)/shard_map/pcg/pallas_call | solution.py:514
  92.3 0.0 copy-start
  92.3 1.5 %copy.12 = f32[128,128]{1,0:T(8,128)} copy(f32[128,128]{1,0:T(8,128)} %get-tuple-element.4) | data formatting | bytes 131072
  93.8 0.0 copy-done
  93.8 0.6 copy.13
Async XLA Ops:
  92.3 1.5 %copy-start = (f32[128,128]{1,0:T(8,128)S(1)}, f32[128,128]{1,0:T(8,128)}, u32[]{:S(2)}) copy-start(f32[128,128]{1,0:T(8,128)} %get-tuple-element.5) | copy-start | bytes 196612

commit v4 on v3

--- a/solution.py
+++ b/solution.py
@@ -51,16 +51,29 @@
 
 def kernel(
     dims,
-    rhs_ref, surf_ref, east_ref, north_ref, neast_ref, nwest_ref, land_ref, fold_ref,
+    rhs_in, surf_in, east_in, north_in, neast_in, nwest_in, land_in, fold_ref,
     x_ref, r_ref,
+    rhs_ref, surf_ref, east_ref, north_ref, neast_ref, nwest_ref, land_ref, insem,
     W, D, fac, invp, resp, g_ref, u, w, m, p, s, q, z, y, nf, vf,
-    coef, fw, perm, me, ye, ge, dots, scal,
-    e1s, e1r, e2s, e2r, e3s, e3r, cs, cr, hs, hr, gs, gr, ls, lr,
-    e1sem, e2sem, e3sem, csem, hsem, gsem, lsem,
+    coef, fw, fx, perm, me, ye, ge, dots, scal,
+    coefg, fwg, mg, yg, mge, yge,
+    e1s, e1r, e2s, e2r, e3s, e3r, e4s, e4r, cs, cr, gs, gr, ls, lr,
+    e1sem, e2sem, e3sem, e4sem, csem, gsem, lsem,
 ):
     NL, NX, NZ, NC = dims
     NZC, NLON = NZ * NC, NX * NZ * NC
     n, cols = rhs_ref.shape
+    loads = [
+        pltpu.make_async_copy(src, dst, insem.at[i])
+        for i, (src, dst) in enumerate(
+            (
+                (land_in, land_ref), (north_in, north_ref), (neast_in, neast_ref), (nwest_in, nwest_ref),
+                (east_in, east_ref), (surf_in, surf_ref), (rhs_in, rhs_ref),
+            )
+        )
+    ]
+    for load in loads:
+        load.start()
     lat, xx, zz, cc = (lax.axis_index(a) for a in ("lat",) + LON)
     lon = xx * NZC + zz * NC + cc
 
@@ -69,11 +82,22 @@
 
     east_dev = lon_device(lax.rem(lon + 1, NLON))
     west_dev = lon_device(lax.rem(lon + NLON - 1, NLON))
-    plane_devs = [lon_device(lax.rem(lon + d, NLON)) for d in range(1, NLON)]
+    offsets = [(a, b, c) for a in range(NX) for b in range(NZ) for c in range(NC)]
+    offsets.sort(key=lambda o: (-(min(o[0], NX - o[0]) + min(o[1], NZ - o[1])), -o[2]))
+    plane_devs = [
+        (lat, lax.rem(xx + a, NX), lax.rem(zz + b, NZ), lax.rem(cc + c, NC))
+        for a, b, c in offsets
+        if (a, b, c) != (0, 0, 0)
+    ]
     lat_devs = [(lax.rem(lat + d, NL), xx, zz, cc) for d in range(1, NL)]
 
     barrier = pltpu.get_barrier_semaphore()
-    greet = plane_devs + lat_devs
+    side_devs = []
+    for d in range(1, NL + 1):
+        at = lax.rem(lat + d, NL)
+        side_devs.append((2, (at,) + west_dev[1:]))
+        side_devs.append((0, (at,) + east_dev[1:]))
+    greet = plane_devs + lat_devs + [dev for _, dev in side_devs[:-2]]
     for dev in greet:
         pl.semaphore_signal(barrier, inc=1, device_id=dev, device_id_type=MESH)
 
@@ -128,6 +152,8 @@
             )
         return values * invp[...]
 
+    for load in loads:
+        load.wait()
     ocean = land_ref[...].astype(F32)
     raw_north = north_ref[...]
     east = east_ref[...]
@@ -155,6 +181,29 @@
     block_hi = fold0 // cols
     block_lo = jnp.where(block_hi == 0, NLON - 1, block_hi - 1)
     source_block = jnp.where(lane_row <= offset, block_hi, block_lo)
+    fold_w = jnp.where(fold0 == NLON * cols - 1, 0, fold0 + 1)
+    block_w, lane_w = fold_w // cols, fold_w & (cols - 1)
+    side_block = jnp.where(lane_row == lane_w, block_w, jnp.where(lane_row == offset, block_lo, -1))
+    lon_w, lon_e = lax.rem(lon + NLON - 1, NLON), lax.rem(lon + 1, NLON)
+
+    def facing_rows(get):
+        parts = [[jnp.zeros((2, cols), F32)] * 4 for _ in range(3)]
+        for j in range(NLON):
+            got = get(j)
+            for part, value in zip(
+                parts,
+                (
+                    jnp.where(source_block == j, got, 0.0),
+                    jnp.where(side_block == j, got, 0.0),
+                    got,
+                ),
+            ):
+                part[j % 4] = part[j % 4] + value
+        return [(part[0] + part[1]) + (part[2] + part[3]) for part in parts]
+
+    def pick(row, lane):
+        value = jnp.sum(jnp.where(lane_row == lane, row, 0.0), axis=1, keepdims=True)
+        return jnp.broadcast_to(value, (1, cols))
     perm[...] = jnp.where(row_ids == (fold & (cols - 1)), 1.0, 0.0)
 
     def facing(row):
@@ -326,22 +375,33 @@
     g_ref[...] = is_top * resp1 + g_rows[0] * resp0 + g_rows[1] * resp1
     ge[...] = stacked(g_rows)
 
-    take(cr.at[pl.ds(0, NLON - 1)], csem.at[1])
-    partner = jnp.zeros((2, cols), F32)
-    for j in range(NLON):
-        partner = partner + jnp.where(source_block == j, cr[j], 0.0)
-    fold_open = 0.5 * (top_rows[5:6] + facing(partner[0:1]))
-    fw[...] = jnp.broadcast_to(fold_open * top_rows[1:2] * facing(partner[1:2]), fw.shape)
-    D[...] = D[...] + jnp.where(top_mask, ocean * fold_open, 0.0)
+    turned = [jnp.transpose(x) for x in (resp0, resp1, g_ref[...], u0)]
+    shared = rows[:2] + g_rows[:2] + [coef_south, coef_north]
+    e4s[0] = jnp.concatenate([last(x) for x in turned] + shared, axis=0)
+    e4s[1] = jnp.concatenate([first(x) for x in turned] + shared, axis=0)
+    start(e4s.at[0], e4r.at[0], e4sem.at[0], e4sem.at[1], east_dev)
+    start(e4s.at[1], e4r.at[1], e4sem.at[2], e4sem.at[3], west_dev)
 
     for ref, sem in (
         (e1r.at[pl.ds(0, NL - 1)], e1sem.at[0]),
-        (cr.at[pl.ds(0, NLON - 1)], csem.at[0]),
         (e2s.at[0], e2sem.at[0]),
         (e2s.at[1], e2sem.at[2]),
         (e3r.at[pl.ds(0, NL - 1)], e3sem.at[0]),
+        (e4s.at[0], e4sem.at[0]),
+        (e4s.at[1], e4sem.at[2]),
     ):
         take(ref, sem)
+    take(e4r.at[0], e4sem.at[1])
+    take(e4r.at[1], e4sem.at[3])
+    for side in range(2):
+        mg[side : side + 1] = e4r[side, 3:4]
+        mge[2 * side : 2 * side + 2] = e4r[side, 4:6]
+        for b in range(NL):
+            for i in range(2):
+                at = 8 + i * order + 2 * b
+                coefg[side, i, b] = e4r[side, at : at + 2]
+    yg[...] = jnp.zeros(yg.shape, F32)
+    yge[...] = jnp.zeros(yge.shape, F32)
 
     def gather_top(par, top_row):
         mine = jnp.concatenate([top_row, dots[0:1]], axis=0)
@@ -379,11 +439,6 @@
         h = m[...]
         he = me[...]
         south, north_row = he[0:1], he[1:2]
-        h_t = jnp.transpose(h)
-        hs[par, 0] = jnp.concatenate([last(h_t), south, north_row, north_row], axis=0)
-        hs[par, 1] = jnp.concatenate([first(h_t), south, north_row, north_row], axis=0)
-        start(hs.at[par, 0], hr.at[par, 0], hsem.at[0, par], hsem.at[2, par], east_dev)
-        start(hs.at[par, 1], hr.at[par, 1], hsem.at[1, par], hsem.at[3, par], west_dev)
         gather_top(par, he[2:3])
 
         rr, uu, ww, ss, qq, zz_ = r_ref[...], u[...], w[...], s[...], q[...], z[...]
@@ -391,48 +446,94 @@
             0: total(rr * uu), 1: total(ww * uu), 2: total(ss * uu), 3: total(ww * h), 4: total(ss * h),
             5: total(ss * qq), 7: total(zz_ * h), 8: total(zz_ * qq),
         }
-        take(hr.at[par, 0], hsem.at[2, par])
-        take(hr.at[par, 1], hsem.at[3, par])
-        west = hr[par, 0]
-        eastern = hr[par, 1]
-        h_w = from_west(h, west[0:1])
-        h_e = from_east(h, eastern[0:1])
+        hge = mge[...]
+        h_w = from_west(h, mg[0:1])
+        h_e = from_east(h, mg[1:2])
         acc = D[...] * h - W[0] * h_e - W[1] * h_w
         acc = acc - W[2] * above(h, north_row) - W[3] * below(h, south)
-        acc = acc - W[4] * above(h_e, row_from_east(north_row, eastern[2:3]))
-        acc = acc - W[5] * below(h_w, row_from_west(south, west[1:2]))
-        acc = acc - W[6] * above(h_w, row_from_west(north_row, west[2:3]))
-        acc = acc - W[7] * below(h_e, row_from_east(south, eastern[1:2]))
+        acc = acc - W[4] * above(h_e, row_from_east(north_row, hge[3:4]))
+        acc = acc - W[5] * below(h_w, row_from_west(south, hge[0:1]))
+        acc = acc - W[6] * above(h_w, row_from_west(north_row, hge[1:2]))
+        acc = acc - W[7] * below(h_e, row_from_east(south, hge[2:3]))
         nf[...] = acc
         local = local_solve(acc)
         sums[6] = total(acc * h)
         sums_row = packed(sums)
-        mine = jnp.concatenate([first(local), last(local), sums_row, sums_row], axis=0)
-        ls[par] = mine
-        lr[par, lat] = mine
+        local_t = jnp.transpose(local)
+        head = [first(local), last(local), sums_row]
+        eastward = jnp.concatenate(head + [last(local_t)], axis=0)
+        ls[par, 0] = eastward
+        ls[par, 1] = jnp.concatenate(head + [first(local_t)], axis=0)
+        lr[par, 1, lat] = eastward
+        for side, dev in side_devs:
+            start(
+                ls.at[par, side // 2], lr.at[par, side, lat],
+                lsem.at[side // 2, par], lsem.at[2 + side, par], dev,
+            )
         for dev in lat_devs:
-            start(ls.at[par], lr.at[par, lat], lsem.at[0, par], lsem.at[1, par], dev)
-
-        take(lr.at[par, pl.ds(0, NL - 1)], lsem.at[1, par])
-        rows = outer_rows(lambda b: lr[par, b, 0:2])
-        sums_row = lr[par, 0, 2:3]
+            start(ls.at[par, 0], lr.at[par, 1, lat], lsem.at[5, par], lsem.at[3, par], dev)
+
+        take(lr.at[par, 1, pl.ds(0, NL - 1)], lsem.at[3, par])
+        rows = outer_rows(lambda b: lr[par, 1, b, 0:2])
+        sums_row = lr[par, 1, 0, 2:3]
         for b in range(1, NL):
-            sums_row = sums_row + lr[par, b, 2:3]
+            sums_row = sums_row + lr[par, 1, b, 2:3]
+        take(lr.at[par, 0], lsem.at[2, par])
+        take(lr.at[par, 2], lsem.at[4, par])
+        side_rows = []
+        for side in range(2):
+            for i in range(2):
+                line = coefg[side, i, 0] * lr[par, 2 * side, 0, 0:2]
+                for b in range(1, NL):
+                    line = line + coefg[side, i, b] * lr[par, 2 * side, b, 0:2]
+                side_rows.append(jnp.sum(line, axis=0, keepdims=True))
         vf[...] = with_ends(local, rows)
 
         take(gr.at[par, pl.ds(0, NLON - 1)], gsem.at[1, par])
-        picked = [jnp.zeros((2, cols), F32) for _ in range(4)]
-        summed = [jnp.zeros((2, cols), F32) for _ in range(4)]
-        for j in range(NLON):
-            got = gr[par, j]
-            picked[j % 4] = picked[j % 4] + jnp.where(source_block == j, got, 0.0)
-            summed[j % 4] = summed[j % 4] + got
-        row = ((picked[0] + picked[1]) + (picked[2] + picked[3]))[0:1]
-        whole_sums = ((summed[0] + summed[1]) + (summed[2] + summed[3]))[1:2]
-        f = fw[0:1] * facing(row)
+
+        @pl.when(k == 0)
+        def _():
+            take(cr.at[pl.ds(0, NLON - 1)], csem.at[1])
+            partner, beside, _ = facing_rows(lambda j: cr[j])
+            fold_open = 0.5 * (cs[0:1] + facing(partner[0:1]))
+            fw[0:1] = fold_open * cs[1:2] * facing(partner[1:2])
+            fx[0:1] = fold_open * cs[1:2]
+            D[...] = D[...] + jnp.where(top_mask, fold_open * cs[1:2], 0.0)
+            for side, (at, lane, facing_lane) in enumerate(
+                ((lon_w, cols - 1, lane_w), (lon_e, 0, offset))
+            ):
+                own = cr[at]
+                opened = 0.5 * (pick(own[0:1], lane) + pick(beside[0:1], facing_lane))
+                opened = opened * pick(own[1:2], lane)
+                fwg[side : side + 1] = opened * pick(beside[1:2], facing_lane)
+                fwg[2 + side : 3 + side] = opened
+            take(cr.at[pl.ds(0, NLON - 1)], csem.at[0])
+
+        row, beside, whole_sums = facing_rows(lambda j: gr[par, j])
+        row, beside, whole_sums = row[0:1], beside[0:1], whole_sums[1:2]
+        side_f = [
+            fwg[0:1] * pick(beside, lane_w)
+            - fwg[2:3] * pick(gr[par, lon_w, 0:1], cols - 1),
+            fwg[1:2] * pick(beside, offset) - fwg[3:4] * pick(gr[par, lon_e, 0:1], 0),
+        ]
+        f = fw[0:1] * facing(row) - fx[0:1] * he[2:3]
         dots[0:1] = sums_row - jnp.where(lane_row == 6, total(f * he[2:3]), 0.0)
         v = vf[...] - g_ref[...] * f
         ve = stacked(rows) - ge[...] * f
+        vg, vge = [], []
+        for side in range(2):
+            south_g, north_g = (x[0:1, cols - 1 : cols] if side == 0 else x[0:1, 0:1]
+                                for x in side_rows[2 * side : 2 * side + 2])
+            vg.append(
+                lr[par, 2 * side, lat, 3:4]
+                + jnp.broadcast_to(south_g, (1, cols)) * e4r[side, 0:1]
+                + jnp.broadcast_to(north_g, (1, cols)) * e4r[side, 1:2]
+                - e4r[side, 2:3] * side_f[side]
+            )
+            for i in range(2):
+                vge.append(side_rows[2 * side + i] - e4r[side, 6 + i : 7 + i] * side_f[side])
+        vg = jnp.concatenate(vg, axis=0)
+        vge = jnp.concatenate(vge, axis=0)
         nn = nf[...] - jnp.where(top_mask, f, 0.0)
 
         @pl.when(k == 0)
@@ -440,6 +541,10 @@
             w[...] = nn
             m[...] = v
             me[...] = ve
+            mg[...] = vg
+            mge[...] = vge
+            fx[...] = jnp.zeros(fx.shape, F32)
+            fwg[2:4] = jnp.zeros((2, cols), F32)
 
         @pl.when(k > 0)
         def _():
@@ -454,6 +559,12 @@
             q[...] = q_new
             m[...] = m[...] - alpha * y_new
             me[...] = me[...] - alpha * ye_new
+            yg_new = vg + beta * yg[...]
+            yg[...] = yg_new
+            mg[...] = mg[...] - alpha * yg_new
+            yge_new = vge + beta * yge[...]
+            yge[...] = yge_new
+            mge[...] = mge[...] - alpha * yge_new
             s_new = w[...] + beta * s[...]
             s[...] = s_new
             z_new = nn + beta * z[...]
@@ -465,10 +576,10 @@
             x_ref[...] = x_ref[...] + alpha * p_new
             r_ref[...] = r_ref[...] - alpha * s_new
 
-        take(hs.at[par, 0], hsem.at[0, par])
-        take(hs.at[par, 1], hsem.at[1, par])
         take(gr.at[par, pl.ds(0, NLON - 1)], gsem.at[0, par])
-        take(lr.at[par, pl.ds(0, NL - 1)], lsem.at[0, par])
+        take(lr.at[par, 0], lsem.at[0, par])
+        take(lr.at[par, 2], lsem.at[1, par])
+        take(lr.at[par, 1, pl.ds(0, NL - 1)], lsem.at[5, par])
         return carry
 
     lax.fori_loop(0, ITERS, body, 0)
@@ -494,27 +605,29 @@
     field = lambda *lead: pltpu.VMEM(lead + (n, cols), F32)
     dma = pltpu.SemaphoreType.DMA
     scratch = [
+        *[field() for _ in range(6)], pltpu.VMEM((n, cols), jnp.int32), dma((7,)),
         field(8), field(), field(2 * levels), field(), field(2), field(),
         *[field() for _ in range(8)],
         field(), field(),
-        vmem(3, NL, 2, cols), vmem(8, cols), field(),
+        vmem(3, NL, 2, cols), vmem(8, cols), vmem(8, cols), field(),
         vmem(8, cols), vmem(8, cols), vmem(8, cols), vmem(8, cols), vmem(8, cols),
+        vmem(2, 2, NL, 2, cols), vmem(4, cols), vmem(2, cols), vmem(2, cols), vmem(4, cols), vmem(4, cols),
         vmem(8, cols), vmem(NL, 8, cols),
         vmem(2, 8, cols), vmem(2, 8, cols),
         vmem(8, cols), vmem(NL, 8, cols),
+        vmem(2, 8 + 4 * NL, cols), vmem(2, 8 + 4 * NL, cols),
         vmem(2, cols), vmem(NLON, 2, cols),
-        vmem(2, 2, 4, cols), vmem(2, 2, 4, cols),
         vmem(2, 2, cols), vmem(2, NLON, 2, cols),
-        vmem(2, 4, cols), vmem(2, NL, 4, cols),
-        dma((2,)), dma((4,)), dma((2,)), dma((2,)),
-        dma((4, 2)), dma((2, 2)), dma((2, 2)),
+        vmem(2, 2, 4, cols), vmem(2, 3, NL, 4, cols),
+        dma((2,)), dma((4,)), dma((2,)), dma((4,)), dma((2,)),
+        dma((2, 2)), dma((6, 2)),
     ]
     spec = pl.BlockSpec(memory_space=pltpu.VMEM)
     shape = jax.ShapeDtypeStruct((n, cols), F32)
     return pl.pallas_call(
         functools.partial(kernel, dims),
         out_shape=(shape, shape),
-        in_specs=[spec] * 8,
+        in_specs=[pl.BlockSpec(memory_space=pl.ANY)] * 7 + [spec],
         out_specs=(spec, spec),
         scratch_shapes=scratch,
         compiler_params=pltpu.CompilerParams(collective_id=0, has_side_effects=True),

time: 94.6 us -> 86 us (0.909)
  Pallas kernels: 91.7 us -> 83 us
    pallas_call x1, Pallas kernels: 91.7 us -> 83 us  [shards(): pl.pallas_call(functools.partial(kernel, dims), out_shape=(shape, shape),...]
where the time goes in v4:
time: 86 us; the launch traced here: 85.8 us
  Pallas kernels  83 us (97%)
  local copies, waits for them, and re-layouts  2.14 us (2%)
    pallas_call x1, Pallas kernels, shards(): pl.pallas_call(functools.partial(kernel, dims), out_shape=(shape, shape),...  83 us
    unnamed x4, local copies, waits for them, and re-layouts  2.14 us

profile of v4, /device:TPU:1, one launch (start us, length us, event | category | flops | bytes accessed | tf_op | source)
XLA Modules:
  0.0 85.8 jit_solution(3047776823569928851)
XLA Ops:
  0.6 83.0 %pcg.1 = (f32[128,128]{1,0:T(8,128)}, f32[128,128]{1,0:T(8,128)}) custom-call(f32[128,128]{1,0:T(8,128)} %rhs_in.1, f32[128,128]{1,0:T(8,128)} %surf_in.1, f32[128,128]{1,0:T(8,128)} %east_in.1, f32[128,128]{1,0:T(8,128)} %north_in.1, f32[128,128]{1,0:T(8,128)} %neast_in.1, f32[128,128]{1,0:T(8,128)} %nwest_in.1, s32[128,128]{1,0:T(8,128)} %land_in.1, ...), custom_call_target="tpu_custom_call" | custom-call | tf_op jit(solution)/shard_map/pcg/pallas_call | solution.py:627
  83.6 0.0 copy-start
  83.7 1.5 %copy.12 = f32[128,128]{1,0:T(8,128)} copy(f32[128,128]{1,0:T(8,128)} %get-tuple-element.4) | data formatting | bytes 131072
  85.2 0.0 copy-done
  85.2 0.6 copy.13
Async XLA Ops:
  83.6 1.5 %copy-start = (f32[128,128]{1,0:T(8,128)S(1)}, f32[128,128]{1,0:T(8,128)}, u32[]{:S(2)}) copy-start(f32[128,128]{1,0:T(8,128)} %get-tuple-element.5) | copy-start | bytes 196612
